TPU v7x, 32 devices: a whole 2x2x4 slice. The times are simulated.
32 devices in a mesh: comp: 8 (over z, x), gy: 2 (over y), gx: 2 (over core).
Axes of the slice: x: 2, y: 2, z: 4, core: 2. Of those that a mesh axis runs over, the one named last changes fastest.
Arguments:
- flow_fields: float32 [4, 6, 256, 384], P(None, None, ('comp', 'gy', 'gx')), may hold values from -6 to 6
- chlorophyll_lag: float32 [6, 256, 384], P(None, ('comp', 'gy', 'gx')), may hold values from 0.1 to 3
- tracers: float32 [16, 6, 256, 128], P(None, None, ('comp', 'gy', 'gx')), may hold values from -6 to 6
- forcing: float32 [4, 6, 256, 128], P(None, None, ('comp', 'gy', 'gx')), may hold values from -6 to 6
- ocean_mask: int32 [64, 384], replicated, may hold values 0 or 1
- bottom: int32 [64, 384], replicated, may hold values from 1 to 6
- reaction: float32 [16, 16], replicated, may hold values from -1.5 to 0.1
Outputs:
- flow_out: float32 [4, 6, 256, 384], P(None, None, ('comp', 'gy', 'gx'))
- light_out: float32 [6, 256, 384], P(None, ('comp', 'gy', 'gx'))
- tracers_out: float32 [16, 6, 256, 128], P(None, None, ('comp', 'gy', 'gx'))
- forcing_out: float32 [4, 6, 256, 128], P(None, None, ('comp', 'gy', 'gx'))
All inputs are finite; a program needn't handle non-finite values.
Results may differ from a plain program's by a relative error of at most 0.0002.
Values sent between devices are 32-bit elements; how exact they have to be, the bound alone decides.
A program may use at most 64 MiB of HBM per device.

v0:
```python
import functools
import math

import jax
import jax.numpy as jnp
from jax import lax
from jax.experimental import pallas as pl
from jax.experimental.pallas import tpu as pltpu
from jax.sharding import PartitionSpec as P

SUB = 4
MESH = pl.DeviceIdType.MESH
AXES = ("comp", "gy", "gx")


def substep(state, above, heat, wet, first, last):
    u, v, t, s = state
    rows, cols = u.shape
    p = above + 0.2 * (s - t)

    def row_next(x):
        return pltpu.roll(x, rows - 1, 0)

    def row_prev(x):
        return pltpu.roll(x, 1, 0)

    def col_next(x):
        return jnp.where(last, 0.0, pltpu.roll(x, cols - 1, 1))

    def col_prev(x):
        return jnp.where(first, 0.0, pltpu.roll(x, 1, 1))

    um, up, vm, vp = 1.0 - u, 1.0 + u, 1.0 - v, 1.0 + v
    new_u = 0.79 * u + 0.1 * v + 0.05 * (row_next(u - p) + row_prev(u + p) + col_next(u) + col_prev(u))
    new_v = 0.79 * v - 0.1 * u + 0.05 * (row_next(v) + row_prev(v) + col_next(v - p) + col_prev(v + p))
    new_t = 0.8 * t + 0.05 * (row_next(t * um) + row_prev(t * up) + col_next(t * vm) + col_prev(t * vp)) + heat
    new_s = 0.8 * s + 0.05 * (row_next(s * um) + row_prev(s * up) + col_next(s * vm) + col_prev(s * vp))
    return tuple(jnp.where(wet, x, 0.0) for x in (new_u, new_v, new_t, new_s)), p


def kernel(sizes, flow_h, chl_h, tracers_h, forcing_h, ocean_h, bottom_h, reaction,
           flow_out, light_out, tracers_out, forcing_out,
           flow, chl, tracers, forcing, ocean, bottom, load_s, state, pigment, depth, total, optical, light, total2, optical2, light2, pig16,
           drive_send, drive_row_send, drive2_send,
           row_send, col_send, row_recv, col_recv, row_send2, col_send2, row_recv2, col_recv2,
           held, pig_mid_s, pig_lo_s, pig_hi_s, pig_mid, pig_lo, pig_hi,
           drive, drive_row, drive2, light_s, light_r,
           flow_ss, flow_rs, chl_ss, chl_rs, row_ss, row_rs, col_ss, col_rs,
           row2_ss, row2_rs, col2_ss, col2_rs, pig_ss, pig_rs,
           drive_ss, drive_rs, drow_ss, drow_rs, drive2_ss, drive2_rs, light_ss, light_rs):
    n_comp, n_gy, n_gx = sizes
    grid = n_gy * n_gx
    every = n_comp * grid
    group = every // 4
    levels, tile, cols = chl.shape
    nt = tracers.shape[0]
    yt = tracers.shape[3]
    position = (lax.axis_index("comp") * grid + lax.axis_index("gy") * n_gx + lax.axis_index("gx")).astype(jnp.int32)
    moved = lax.rem(position + 1, jnp.int32(every))
    strip = lax.rem(moved, jnp.int32(group))
    section = lax.div(moved, jnp.int32(group))
    is_dyn = section == 3
    has_lo = strip > 0
    has_hi = strip < group - 1
    has_left = section > 0
    has_right = section < 2

    def dev(sec, row):
        pos = lax.rem(sec * group + row + (every - 1), jnp.int32(every))
        return (lax.div(pos, jnp.int32(grid)), lax.rem(lax.div(pos, jnp.int32(n_gx)), jnp.int32(n_gy)),
                lax.rem(pos, jnp.int32(n_gx)))

    def remote(src, dst, send_sem, recv_sem, target):
        return pltpu.make_async_remote_copy(src_ref=src, dst_ref=dst, send_sem=send_sem, recv_sem=recv_sem,
                                            device_id=target, device_id_type=MESH)

    three = jnp.int32(3)
    barrier = pltpu.get_barrier_semaphore()

    def load(i, src, dst):
        return pltpu.make_async_copy(src, dst, load_s.at[i])

    def mask_loads(part, offset):
        begin = pl.multiple_of(jnp.clip(strip + offset, 0, group - 1) * tile, tile)
        return (load(2 + 2 * part, ocean_h.at[pl.ds(begin, tile), :], ocean.at[part]),
                load(3 + 2 * part, bottom_h.at[pl.ds(begin, tile), :], bottom.at[part]))

    def greet(sec, row):
        pl.semaphore_signal(barrier, inc=1, device_id=dev(sec, row), device_id_type=MESH)

    sides = ((0, -1, has_lo), (1, 1, has_hi))
    lo_n = has_lo.astype(jnp.int32)
    hi_n = has_hi.astype(jnp.int32)

    @pl.when(is_dyn)
    def _():
        loads = [load(0, flow_h, flow), load(1, chl_h, chl)]
        for part in range(3):
            loads.extend(mask_loads(part, part - 1))
        for copy in loads:
            copy.start()
        for side, (present, buf) in ((0, (has_lo, pig_lo)), (2, (has_hi, pig_hi))):
            @pl.when(jnp.logical_not(present))
            def _():
                zero_tile = jnp.zeros((levels, tile, cols), jnp.float32)
                for f in range(4):
                    state[f, :, side * tile:(side + 1) * tile, :] = zero_tile
                pigment[:, side * tile:(side + 1) * tile, :] = zero_tile
                buf[...] = jnp.zeros_like(buf)
        for _, offset, present in sides:
            @pl.when(present)
            def _():
                greet(three, strip + offset)
                for sec in range(3):
                    greet(jnp.int32(sec), strip + offset)
        for sec in range(3):
            greet(jnp.int32(sec), strip)
        total[...] = jnp.zeros_like(total)
        total2[...] = jnp.zeros_like(total2)
        optical[...] = jnp.zeros_like(optical)
        optical2[...] = jnp.zeros_like(optical2)
        light[...] = jnp.ones_like(light)
        light2[...] = jnp.ones_like(light2)
        tracers_out[...] = jnp.zeros_like(tracers_out)
        forcing_out[...] = jnp.zeros_like(forcing_out)
        for copy in loads:
            copy.wait()
        pl.semaphore_wait(barrier, 3 + 4 * lo_n + 4 * hi_n)

        def halo_copies(k, side, offset):
            place = pl.ds(2 * tile if side == 0 else 0, tile)
            target = dev(three, strip + offset)
            return (remote(flow.at[:, k], state.at[:, k, place, :], flow_ss.at[side, k], flow_rs.at[1 - side, k], target),
                    remote(chl.at[k], pigment.at[k, place, :], chl_ss.at[side, k], chl_rs.at[1 - side, k], target))

        def halo_arrivals(k, side, offset):
            place = pl.ds(0 if side == 0 else 2 * tile, tile)
            target = dev(three, strip + offset)
            return (remote(flow.at[:, k], state.at[:, k, place, :], flow_ss.at[side, k], flow_rs.at[side, k], target),
                    remote(chl.at[k], pigment.at[k, place, :], chl_ss.at[side, k], chl_rs.at[side, k], target))

        def drive_copies(k, sec):
            target = dev(jnp.int32(sec), strip)
            return (remote(drive_send.at[k, sec], drive.at[k], drive_ss.at[sec, k], drive_rs.at[k], target),
                    remote(drive_row_send.at[k, sec], drive_row.at[k], drow_ss.at[sec, k], drow_rs.at[k], target))

        def drive2_copy(k, sec):
            return remote(drive2_send.at[k, sec], drive2.at[k], drive2_ss.at[sec, k], drive2_rs.at[k],
                          dev(jnp.int32(sec), strip))

        for side, offset, present in sides:
            @pl.when(present)
            def _():
                @pl.loop(0, levels)
                def _(k):
                    for copy in halo_copies(k, side, offset):
                        copy.start()

        for part, present in ((0, has_lo), (1, None), (2, has_hi)):
            deep = jnp.where(ocean[part] == 1, bottom[part], 0)
            if present is not None:
                deep = deep * present.astype(jnp.int32)
            depth[part * tile:(part + 1) * tile, :] = deep
        for f in range(4):
            state[f, :, tile:2 * tile, :] = flow[f]
        pigment[:, tile:2 * tile, :] = chl[...]

        def edges(rows):
            lane = lax.broadcasted_iota(jnp.int32, (rows, cols), 1)
            return lane == 0, lane == cols - 1

        lane_t = lax.broadcasted_iota(jnp.int32, (tile, yt), 1)

        @pl.loop(0, levels)
        def _(k):
            for side, offset, present in sides:
                @pl.when(present)
                def _():
                    for copy in halo_arrivals(k, side, offset):
                        copy.wait_recv()
            first, last = edges(3 * tile)
            opt = optical[...] + (0.05 + 0.3 * pigment[k])
            lower = jnp.exp(-opt)
            heat = 0.5 * (light[...] - lower)
            optical[...] = opt
            light[...] = lower
            wet = k < depth[...]
            now = tuple(state[f, k] for f in range(4))
            sum_u = None
            for n in range(SUB):
                now, p = substep(now, total[n], heat, wet, first, last)
                total[n] = p
                sum_u = now[0] if n == 0 else sum_u + now[0]
                sum_v = now[1] if n == 0 else sum_v + now[1]
            for f in range(4):
                state[f, k] = now[f]
            mean_u = sum_u * (1.0 / SUB)
            mean_v = sum_v[tile:2 * tile] * (1.0 / SUB)
            mix = 0.1 * now[2][tile:2 * tile] - 0.05 * now[3][tile:2 * tile]
            zero = jnp.zeros((tile, yt), jnp.float32)
            for sec in range(3):
                here = slice(sec * yt, (sec + 1) * yt)
                before = mean_v[:, (sec - 1) * yt:sec * yt] if sec > 0 else zero
                after = mean_v[:, (sec + 1) * yt:(sec + 2) * yt] if sec < 2 else zero
                drive_send[k, sec, 0] = mean_u[tile:2 * tile, here]
                drive_send[k, sec, 1] = mean_v[:, here]
                drive_send[k, sec, 2] = mix[:, here]
                drive_send[k, sec, 3] = jnp.where(lane_t == yt - 1, before, after)
                drive_row_send[k, sec, 0] = mean_u[tile - 1:tile, here]
                drive_row_send[k, sec, 1] = mean_u[2 * tile:2 * tile + 1, here]
            for sec in range(3):
                for copy in drive_copies(k, sec):
                    copy.start()

        half = tile // 2
        wide = 2 * tile

        @pl.loop(0, levels)
        def _(k):
            for sec in range(3):
                origin = dev(jnp.int32(sec), strip)
                remote(pig_mid_s.at[k], pig_mid.at[sec, k], pig_ss.at[1, k], pig_rs.at[sec, 1, k], origin).wait_recv()
                for part, buf_s, buf, offset, present in ((0, pig_hi_s, pig_lo, -1, has_lo), (2, pig_lo_s, pig_hi, 1, has_hi)):
                    @pl.when(present)
                    def _():
                        origin = dev(jnp.int32(sec), strip + offset)
                        remote(buf_s.at[k], buf.at[sec, k], pig_ss.at[part, k], pig_rs.at[sec, part, k], origin).wait_recv()
                here = slice(sec * yt, (sec + 1) * yt)
                pig16[0:half, here] = pig_lo[sec, k]
                pig16[half:half + tile, here] = pig_mid[sec, k]
                pig16[half + tile:wide, here] = pig_hi[sec, k]
            first, last = edges(wide)
            opt = optical2[...] + (0.05 + 0.3 * pig16[...])
            lower = jnp.exp(-opt)
            heat = 0.5 * (light2[...] - lower)
            optical2[...] = opt
            light2[...] = lower
            wet = k < depth[half:half + wide, :]
            now = tuple(state[f, k, half:half + wide, :] for f in range(4))
            sum_u = None
            for n in range(SUB):
                now, p = substep(now, total2[n], heat, wet, first, last)
                total2[n] = p
                sum_u = now[0] if n == 0 else sum_u + now[0]
                sum_v = now[1] if n == 0 else sum_v + now[1]
            own = slice(half, half + tile)
            mean_u = sum_u[own] * (1.0 / SUB)
            mean_v = sum_v[own] * (1.0 / SUB)
            ends = tuple(x[own] for x in now)
            for sec in range(3):
                here = slice(sec * yt, (sec + 1) * yt)
                drive2_send[k, sec, 0] = mean_u[:, here]
                drive2_send[k, sec, 1] = mean_v[:, here]
                drive2_send[k, sec, 2] = ends[2][:, here]
                drive2_send[k, sec, 3] = ends[3][:, here]
            for sec in range(3):
                drive2_copy(k, sec).start()
            for f in range(4):
                flow_out[f, k] = ends[f]

        @pl.loop(0, levels)
        def _(k):
            for sec in range(3):
                remote(light_s.at[k], light_r.at[sec, k], light_ss.at[k], light_rs.at[sec, k],
                       dev(jnp.int32(sec), strip)).wait_recv()
                light_out[k, :, sec * yt:(sec + 1) * yt] = light_r[sec, k]
            for side, offset, present in sides:
                @pl.when(present)
                def _():
                    for copy in halo_copies(k, side, offset):
                        copy.wait_send()
            for sec in range(3):
                for copy in drive_copies(k, sec):
                    copy.wait_send()
                drive2_copy(k, sec).wait_send()

    @pl.when(jnp.logical_not(is_dyn))
    def _():
        loads = [load(0, tracers_h, tracers), load(1, forcing_h, forcing)]
        loads.extend(mask_loads(1, 0))
        for copy in loads:
            copy.start()
        for side, present, bufs in ((0, has_lo, (row_recv, row_recv2)), (1, has_hi, (row_recv, row_recv2)),
                                    (0, has_left, (col_recv, col_recv2)), (1, has_right, (col_recv, col_recv2))):
            @pl.when(jnp.logical_not(present))
            def _():
                for buf in bufs:
                    buf[side] = jnp.zeros(buf.shape[1:], jnp.float32)
        for _, offset, present in sides:
            @pl.when(present)
            def _():
                greet(section, strip + offset)
                greet(three, strip + offset)
        greet(three, strip)
        beside = ((0, -1, has_left), (1, 1, has_right))
        for _, offset, present in beside:
            @pl.when(present)
            def _():
                greet(section + offset, strip)

        lane = lax.broadcasted_iota(jnp.int32, (tile, yt), 1)
        row = lax.broadcasted_iota(jnp.int32, (tile, yt), 0)
        pair = lax.div(lane, jnp.int32(2))
        odd = lax.rem(lane, jnp.int32(2)) == 1

        flow_out[...] = jnp.zeros_like(flow_out)
        light_out[...] = jnp.zeros_like(light_out)
        for copy in loads:
            copy.wait()

        def pack(items):
            packed = jnp.zeros((tile, yt), jnp.float32)
            for i, x in enumerate(items):
                packed = jnp.where(pair == i, pltpu.roll(x, 2 * i + 1, 1), packed)
            return packed

        @pl.loop(0, levels)
        def _(k):
            items = [tracers[i, k] for i in range(nt)]
            col_send[k] = pack(items + [forcing[1, k]])
            for i, x in enumerate(items + [forcing[0, k]]):
                row_send[0, k, i] = x[0:1]
                row_send[1, k, i] = x[tile - 1:tile]

        left = pl.multiple_of(section * yt, yt)
        deep = jnp.where(ocean[1, :, pl.ds(left, yt)] == 1, bottom[1, :, pl.ds(left, yt)], 0)
        pl.semaphore_wait(barrier, 1 + 2 * lo_n + 2 * hi_n + has_left.astype(jnp.int32) + has_right.astype(jnp.int32))

        def row_copy(side, offset, arriving, s_buf, r_buf, ss, rs):
            at = side if arriving else 1 - side
            return remote(s_buf.at[side], r_buf.at[at], ss.at[side], rs.at[at], dev(section, strip + offset))

        def col_copy(side, offset, arriving, s_buf, r_buf, ss, rs):
            at = side if arriving else 1 - side
            return remote(s_buf, r_buf.at[at], ss.at[side], rs.at[at], dev(section + offset, strip))

        exchange_a = ((sides, row_copy, (row_send, row_recv, row_ss, row_rs)),
                      (beside, col_copy, (col_send, col_recv, col_ss, col_rs)))
        exchange_b = ((sides, row_copy, (row_send2, row_recv2, row2_ss, row2_rs)),
                      (beside, col_copy, (col_send2, col_recv2, col2_ss, col2_rs)))

        def run(exchange, arriving, what):
            for places, make, bufs in exchange:
                for side, offset, present in places:
                    @pl.when(present)
                    def _():
                        copy = make(side, offset, arriving, *bufs)
                        if what == "start":
                            copy.start()
                        elif what == "recv":
                            copy.wait_recv()
                        else:
                            copy.wait_send()

        run(exchange_a, False, "start")
        run(exchange_a, True, "recv")

        def tracer_step(k, cs, u, v, growth, u_lo, u_hi, v_edge, rows_of, packed):
            um, up, vm, vp = 1.0 - u, 1.0 + u, 1.0 - v, 1.0 + v
            hi_m, lo_p = 1.0 - u_hi, 1.0 + u_lo
            edge_m, edge_p = 1.0 - v_edge, 1.0 + v_edge
            wet = k < deep
            out = []
            for i in range(nt):
                c = cs[i]
                react = reaction[i, 0] * cs[0]
                for b in range(1, nt):
                    react = react + reaction[i, b] * cs[b]
                nxt = jnp.where(row == tile - 1, rows_of[1, k, i] * hi_m, pltpu.roll(c * um, tile - 1, 0))
                prv = jnp.where(row == 0, rows_of[0, k, i] * lo_p, pltpu.roll(c * up, 1, 0))
                edge = pltpu.roll(packed, yt - (2 * i + 1), 1)
                rgt = pltpu.roll(jnp.where(lane == 0, edge * edge_m, c * vm), yt - 1, 1)
                lft = pltpu.roll(jnp.where(lane == yt - 1, edge * edge_p, c * vp), 1, 1)
                out.append(jnp.where(wet, 0.8 * c + 0.05 * ((nxt + prv) + (rgt + lft)) + growth * react, 0.0))
            return out

        def pig_copies(k):
            return ((None, remote(pig_mid_s.at[k], pig_mid.at[section, k], pig_ss.at[1, k], pig_rs.at[section, 1, k],
                                  dev(three, strip))),
                    (has_lo, remote(pig_lo_s.at[k], pig_hi.at[section, k], pig_ss.at[2, k], pig_rs.at[section, 2, k],
                                    dev(three, strip - 1))),
                    (has_hi, remote(pig_hi_s.at[k], pig_lo.at[section, k], pig_ss.at[0, k], pig_rs.at[section, 0, k],
                                    dev(three, strip + 1))))

        @pl.loop(0, levels)
        def _(k):
            cs = [tracers[i, k] for i in range(nt)]
            packed = jnp.where(odd, col_recv[1, k], col_recv[0, k])
            growth = 0.1 * jnp.exp(0.1 * forcing[2, k] - 0.05 * forcing[3, k])
            v_edge = pltpu.roll(packed, yt - (2 * nt + 1), 1)
            new = tracer_step(k, cs, forcing[0, k], forcing[1, k], growth, row_recv[0, k, nt], row_recv[1, k, nt], v_edge,
                              row_recv, packed)
            pig = 0.25 * (new[0] * new[0] + new[1] * new[1])
            pig_mid_s[k] = pig
            pig_lo_s[k] = pig[:tile // 2]
            pig_hi_s[k] = pig[tile // 2:]
            for present, copy in pig_copies(k):
                if present is None:
                    copy.start()
                else:
                    pl.when(present)(copy.start)
            for i in range(nt):
                held[i, k] = new[i]
                row_send2[0, k, i] = new[i][0:1]
                row_send2[1, k, i] = new[i][tile - 1:tile]
            col_send2[k] = pack(new)

        run(exchange_b, False, "start")
        run(exchange_b, True, "recv")

        def light_copy(k):
            return remote(light_s.at[k], light_r.at[section, k], light_ss.at[k], light_rs.at[section, k], dev(three, strip))

        @pl.loop(0, levels)
        def _(k):
            origin = dev(three, strip)
            remote(drive_send.at[k, 0], drive.at[k], drive_ss.at[0, k], drive_rs.at[k], origin).wait_recv()
            remote(drive_row_send.at[k, 0], drive_row.at[k], drow_ss.at[0, k], drow_rs.at[k], origin).wait_recv()
            cs = [held[i, k] for i in range(nt)]
            packed = jnp.where(odd, col_recv2[1, k], col_recv2[0, k])
            growth = 0.1 * jnp.exp(drive[k, 2])
            new = tracer_step(k, cs, drive[k, 0], drive[k, 1], growth, drive_row[k, 0], drive_row[k, 1], drive[k, 3],
                              row_recv2, packed)
            light_s[k] = 0.25 * (new[0] * new[0] + new[1] * new[1])
            light_copy(k).start()
            for i in range(nt):
                tracers_out[i, k] = new[i]

        @pl.loop(0, levels)
        def _(k):
            remote(drive2_send.at[k, 0], drive2.at[k], drive2_ss.at[0, k], drive2_rs.at[k], dev(three, strip)).wait_recv()
            for f in range(4):
                forcing_out[f, k] = drive2[k, f]
            light_copy(k).wait_send()
            for present, copy in pig_copies(k):
                if present is None:
                    copy.wait_send()
                else:
                    pl.when(present)(copy.wait_send)

        run(exchange_a, False, "send")
        run(exchange_b, False, "send")


def write_out(*refs):
    done = refs[-1]
    copies = [pltpu.make_async_copy(refs[i], refs[4 + i], done.at[i]) for i in range(4)]
    for copy in copies:
        copy.start()
    for copy in copies:
        copy.wait()


def solution(mesh):
    sizes = tuple(mesh.shape[a] for a in AXES)

    def on_device(flow, chl, tracers, forcing, ocean, bottom, reaction):
        levels, tile, cols = chl.shape
        nt, yt = tracers.shape[0], tracers.shape[3]
        f32 = jnp.float32

        def buf(*shape):
            return pltpu.VMEM(shape, f32)

        def sem(*shape):
            return pltpu.SemaphoreType.DMA(shape)

        tall, wide, half = 3 * tile, 2 * tile, tile // 2
        scratch = [
            buf(*flow.shape), buf(*chl.shape), buf(*tracers.shape), buf(*forcing.shape),
            pltpu.VMEM((3, tile, cols), jnp.int32), pltpu.VMEM((3, tile, cols), jnp.int32), sem(8),
            buf(4, levels, tall, cols), buf(levels, tall, cols), pltpu.VMEM((tall, cols), jnp.int32),
            buf(SUB, tall, cols), buf(tall, cols), buf(tall, cols),
            buf(SUB, wide, cols), buf(wide, cols), buf(wide, cols), buf(wide, cols),
            buf(levels, 3, 4, tile, yt), buf(levels, 3, 2, 1, yt), buf(levels, 3, 4, tile, yt),
            buf(2, levels, nt + 1, 1, yt), buf(levels, tile, yt), buf(2, levels, nt + 1, 1, yt), buf(2, levels, tile, yt),
            buf(2, levels, nt, 1, yt), buf(levels, tile, yt), buf(2, levels, nt, 1, yt), buf(2, levels, tile, yt),
            buf(nt, levels, tile, yt),
            buf(levels, tile, yt), buf(levels, half, yt), buf(levels, half, yt),
            buf(3, levels, tile, yt), buf(3, levels, half, yt), buf(3, levels, half, yt),
            buf(levels, 4, tile, yt), buf(levels, 2, 1, yt), buf(levels, 4, tile, yt),
            buf(levels, tile, yt), buf(3, levels, tile, yt),
            sem(2, levels), sem(2, levels), sem(2, levels), sem(2, levels),
            sem(2), sem(2), sem(2), sem(2),
            sem(2), sem(2), sem(2), sem(2),
            sem(3, levels), sem(3, 3, levels),
            sem(3, levels), sem(levels), sem(3, levels), sem(levels), sem(3, levels), sem(levels),
            sem(levels), sem(3, levels),
        ]
        vmem = pl.BlockSpec(memory_space=pltpu.VMEM)
        shapes = [x.shape for x in (flow, chl, tracers, forcing)]
        room = 67043328 - 4 * sum(math.prod(x) for x in shapes) - 2**16
        results = pl.pallas_call(
            functools.partial(kernel, sizes),
            out_shape=[pltpu.VMEM(x, f32) for x in shapes],
            in_specs=[pl.BlockSpec(memory_space=pltpu.HBM)] * 6 + [pl.BlockSpec(memory_space=pltpu.SMEM)],
            out_specs=[vmem] * 4,
            scratch_shapes=scratch,
            compiler_params=pltpu.CompilerParams(collective_id=0, has_side_effects=True, vmem_limit_bytes=room),
        )(flow, chl, tracers, forcing, ocean, bottom, reaction)
        return pl.pallas_call(
            write_out,
            out_shape=[jax.ShapeDtypeStruct(x, f32) for x in shapes],
            in_specs=[vmem] * 4,
            out_specs=[pl.BlockSpec(memory_space=pltpu.HBM)] * 4,
            scratch_shapes=[sem(4)],
            compiler_params=pltpu.CompilerParams(vmem_limit_bytes=4 * 2**20),
        )(*results)

    rows4 = P(None, None, AXES, None)
    rows3 = P(None, AXES, None)
    return jax.shard_map(on_device, mesh=mesh, in_specs=(rows4, rows3, rows4, rows4, P(), P(), P()),
                         out_specs=(rows4, rows3, rows4, rows4), check_vma=False)
```

profile of v0, /device:TPU:1, one launch (start us, length us, event | category | flops | bytes accessed | tf_op | source)
XLA Modules:
  0.0 29.4 jit_solution(5964745423448810947)
XLA Ops:
  0.6 27.8 %shard_map.102 = (f32[4,6,8,384]{3,2,1,0:T(8,128)S(1)}, f32[6,8,384]{2,1,0:T(8,128)S(1)}, f32[16,6,8,128]{3,2,1,0:T(8,128)S(1)}, f32[4,6,8,128]{3,2,1,0:T(8,128)S(1)}) custom-call(f32[4,6,8,384]{3,2,1,0:T(8,128)} %flow_h.1, f32[6,8,384]{2,1,0:T(8,128)} %chl_h.1, f32[16,6,8,128]{3,2,1,0:T(8,128)} %tracers_h.1, f32[4,6,8,128]{3,2,1,0:T(8,128)} %forcing_h.1, ...), custom_call_target="tpu_custom_call" | custom-call | tf_op jit(solution)/shard_map/pallas_call | solution.py:493
  28.4 0.9 %shard_map.103 = (f32[4,6,8,384]{3,2,1,0:T(8,128)}, f32[6,8,384]{2,1,0:T(8,128)}, f32[16,6,8,128]{3,2,1,0:T(8,128)}, f32[4,6,8,128]{3,2,1,0:T(8,128)}) custom-call(f32[4,6,8,384]{3,2,1,0:T(8,128)S(1)} %get-tuple-element.8.refs_0_, f32[6,8,384]{2,1,0:T(8,128)S(1)} %get-tuple-element.9.refs_1_, f32[16,6,8,128]{3,2,1,0:T(8,128)S(1)} %get-tuple-element.10.refs_2_, ...), custom_call_target="tpu_custom_call" | custom-call | tf_op jit(solution)/shard_map/pallas_call | solution.py:501
where the time goes:
time: 29.6 us; the launch traced here: 29.4 us
  Pallas kernels  28.7 us (97%)
  between operations  0.64 us (2%)
    pallas_call x1, Pallas kernels, on_device(): pl.pallas_call(functools.partial(kernel, sizes), out_shape=[pltpu.VMEM(x,...  27.8 us
    pallas_call x1, Pallas kernels, on_device(): pl.pallas_call(write_out, out_shape=[jax.ShapeDtypeStruct(x, f32) for x i...  0.93 us

commit v1 on v0

v1 whole, which is shorter than its diff:
```python
import functools
import math

import jax
import jax.numpy as jnp
from jax import lax
from jax.experimental import pallas as pl
from jax.experimental.pallas import tpu as pltpu
from jax.sharding import PartitionSpec as P

SUB = 4
MESH = pl.DeviceIdType.MESH
AXES = ("comp", "gy", "gx")


def substep(state, above, heat, wet, first, last):
    u, v, t, s = state
    rows, cols = u.shape
    p = above + 0.2 * (s - t)

    def row_next(x):
        return pltpu.roll(x, rows - 1, 0)

    def row_prev(x):
        return pltpu.roll(x, 1, 0)

    def col_next(x):
        return jnp.where(last, 0.0, pltpu.roll(x, cols - 1, 1))

    def col_prev(x):
        return jnp.where(first, 0.0, pltpu.roll(x, 1, 1))

    um, up, vm, vp = 1.0 - u, 1.0 + u, 1.0 - v, 1.0 + v
    new_u = 0.79 * u + 0.1 * v + 0.05 * (row_next(u - p) + row_prev(u + p) + col_next(u) + col_prev(u))
    new_v = 0.79 * v - 0.1 * u + 0.05 * (row_next(v) + row_prev(v) + col_next(v - p) + col_prev(v + p))
    new_t = 0.8 * t + 0.05 * (row_next(t * um) + row_prev(t * up) + col_next(t * vm) + col_prev(t * vp)) + heat
    new_s = 0.8 * s + 0.05 * (row_next(s * um) + row_prev(s * up) + col_next(s * vm) + col_prev(s * vp))
    return tuple(jnp.where(wet, x, 0.0) for x in (new_u, new_v, new_t, new_s)), p


def kernel(sizes, flow_h, chl_h, tracers_h, forcing_h, ocean_h, bottom_h, reaction_h,
           flow_out, light_out, tracers_out, forcing_out,
           flow, chl, tracers, forcing, ocean, bottom, reaction, load_s,
           gflow, gchl, mid, gmid, depth, total, optical, light, total2, optical2, light2, pig,
           drive_send, drive_row_send, drive2_send,
           row_send, col_send, row_recv, col_recv, row_send2, col_send2, row_recv2, col_recv2,
           held, pig_s, drive, drive_row, light_s,
           flow_ss, flow_rs, chl_ss, chl_rs, mid_ss, mid_rs, row_ss, row_rs, col_ss, col_rs,
           row2_ss, row2_rs, col2_ss, col2_rs, pig_ss, pig_rs,
           drive_ss, drive_rs, drow_ss, drow_rs, drive2_ss, drive2_rs, light_ss, light_rs, ready):
    n_comp, n_gy, n_gx = sizes
    grid = n_gy * n_gx
    every = n_comp * grid
    group = every // 4
    levels, tile, cols = chl.shape
    half = tile // 2
    wide = 2 * tile
    nt = tracers.shape[0]
    yt = tracers.shape[3]
    position = (lax.axis_index("comp") * grid + lax.axis_index("gy") * n_gx + lax.axis_index("gx")).astype(jnp.int32)
    moved = lax.rem(position + 1, jnp.int32(every))
    strip = lax.rem(moved, jnp.int32(group))
    section = lax.div(moved, jnp.int32(group))
    is_dyn = section == 3
    has_lo = strip > 0
    has_hi = strip < group - 1
    has_left = section > 0
    has_right = section < 2

    def dev(sec, row):
        pos = lax.rem(sec * group + row + (every - 1), jnp.int32(every))
        return (lax.div(pos, jnp.int32(grid)), lax.rem(lax.div(pos, jnp.int32(n_gx)), jnp.int32(n_gy)),
                lax.rem(pos, jnp.int32(n_gx)))

    def remote(src, dst, send_sem, recv_sem, target):
        return pltpu.make_async_remote_copy(src_ref=src, dst_ref=dst, send_sem=send_sem, recv_sem=recv_sem,
                                            device_id=target, device_id_type=MESH)

    three = jnp.int32(3)
    scope = jax.named_scope
    barrier = pltpu.get_barrier_semaphore()

    def load(i, src, dst):
        return pltpu.make_async_copy(src, dst, load_s.at[i])

    def mask_loads(part, offset):
        begin = pl.multiple_of(jnp.clip(strip + offset, 0, group - 1) * tile, tile)
        return (load(2 + 2 * part, ocean_h.at[pl.ds(begin, tile), :], ocean.at[part]),
                load(3 + 2 * part, bottom_h.at[pl.ds(begin, tile), :], bottom.at[part]))

    def greet(sem, sec, row):
        pl.semaphore_signal(sem, inc=1, device_id=dev(sec, row), device_id_type=MESH)

    sides = ((0, -1, has_lo), (1, 1, has_hi))
    lo_n = has_lo.astype(jnp.int32)
    hi_n = has_hi.astype(jnp.int32)

    def pig_copy(k, sec, part, row):
        from_rows = (pl.ds(0, tile), pl.ds(0, half), pl.ds(half, half))[part]
        to_rows = (pl.ds(0, tile), pl.ds(tile, half), pl.ds(tile + half, half))[part]
        return remote(pig_s.at[k, from_rows], pig.at[sec, k, to_rows], pig_ss.at[part, k], pig_rs.at[sec, part, k],
                      dev(three, row))

    def light_copy(k, sec, begin, row):
        return remote(light_s.at[k], light_out.at[k, :, pl.ds(begin, yt)], light_ss.at[k], light_rs.at[sec, k],
                      dev(three, row))

    @pl.when(is_dyn)
    def _():
        loads = [load(0, flow_h, flow), load(1, chl_h, chl)]
        for part in range(3):
            loads.extend(mask_loads(part, part - 1))
        for copy in loads:
            copy.start()
        for _, offset, present in sides:
            @pl.when(present)
            def _():
                greet(barrier, three, strip + offset)
        for place, present in ((half, has_lo), (0, has_hi)):
            @pl.when(jnp.logical_not(present))
            def _():
                for f in range(4):
                    gflow[f, :, place:place + half, :] = jnp.zeros((levels, half, cols), jnp.float32)
                    gmid[f, :, place:place + half, :] = jnp.zeros((levels, half, cols), jnp.float32)
                gchl[:, place:place + half, :] = jnp.zeros((levels, half, cols), jnp.float32)
                for sec in range(3):
                    pig[sec, :, tile + place:tile + place + half, :] = jnp.zeros((levels, half, yt), jnp.float32)
        total[...] = jnp.zeros_like(total)
        total2[...] = jnp.zeros_like(total2)
        optical[...] = jnp.zeros_like(optical)
        optical2[...] = jnp.zeros_like(optical2)
        light[...] = jnp.ones_like(light)
        light2[...] = jnp.ones_like(light2)
        with scope("d_load"):
            for copy in loads:
                copy.wait()
        with scope("d_bar"):
            pl.semaphore_wait(barrier, 3 + 4 * lo_n + 4 * hi_n)

        def flow_copies(k, side, offset, arriving):
            at = side if arriving else 1 - side
            place = pl.ds(half * (1 - at), half)
            target = dev(three, strip + offset)
            return (remote(flow.at[:, k, place, :], gflow.at[:, k, place, :], flow_ss.at[side, k], flow_rs.at[at, k], target),
                    remote(chl.at[k, place, :], gchl.at[k, place, :], chl_ss.at[side, k], chl_rs.at[at, k], target))

        def mid_copy(k, side, offset, arriving):
            at = side if arriving else 1 - side
            place = pl.ds(half * (1 - at), half)
            return remote(mid.at[:, k, place, :], gmid.at[:, k, place, :], mid_ss.at[side, k], mid_rs.at[at, k],
                          dev(three, strip + offset))

        def drive_copies(k, sec):
            target = dev(jnp.int32(sec), strip)
            return (remote(drive_send.at[k, sec], drive.at[k], drive_ss.at[sec, k], drive_rs.at[k], target),
                    remote(drive_row_send.at[k, sec], drive_row.at[k], drow_ss.at[sec, k], drow_rs.at[k], target))

        def drive2_copy(k, sec):
            return remote(drive2_send.at[k, sec], forcing_out.at[:, k], drive2_ss.at[sec, k], drive2_rs.at[k],
                          dev(jnp.int32(sec), strip))

        @pl.loop(0, levels)
        def _(k):
            for side, offset, present in sides:
                @pl.when(present)
                def _():
                    for copy in flow_copies(k, side, offset, False):
                        copy.start()

        for sec in range(3):
            greet(ready, jnp.int32(sec), strip)
            for _, offset, present in sides:
                @pl.when(present)
                def _():
                    greet(ready, jnp.int32(sec), strip + offset)

        def deep_of(part):
            return jnp.where(ocean[part] == 1, bottom[part], 0)

        row_d = lax.broadcasted_iota(jnp.int32, (tile, cols), 0)
        depth[0:tile, :] = deep_of(1)
        depth[tile:wide, :] = jnp.where(row_d < half, deep_of(2) * hi_n, deep_of(0) * lo_n)
        tracers_out[...] = jnp.zeros_like(tracers_out)
        forcing_out[...] = jnp.zeros_like(forcing_out)

        lane_d = lax.broadcasted_iota(jnp.int32, (wide, cols), 1)
        lane_t = lax.broadcasted_iota(jnp.int32, (tile, yt), 1)

        def phase(k, now, pigment, sums, opt_s, light_ref):
            first, last = lane_d == 0, lane_d == cols - 1
            opt = opt_s[...] + (0.05 + 0.3 * pigment)
            lower = jnp.exp(-opt)
            heat = 0.5 * (light_ref[...] - lower)
            opt_s[...] = opt
            light_ref[...] = lower
            wet = k < depth[...]
            sum_u = None
            for n in range(SUB):
                now, p = substep(now, sums[n], heat, wet, first, last)
                sums[n] = p
                sum_u = now[0] if n == 0 else sum_u + now[0]
                sum_v = now[1] if n == 0 else sum_v + now[1]
            return now, sum_u * (1.0 / SUB), sum_v[0:tile] * (1.0 / SUB)

        @pl.loop(0, levels)
        def _(k):
            with scope("d_halo"):
                for side, offset, present in sides:
                    @pl.when(present)
                    def _():
                        for copy in flow_copies(k, side, offset, True):
                            copy.wait_recv()
            now = tuple(jnp.concatenate([flow[f, k], gflow[f, k]], axis=0) for f in range(4))
            now, mean_u, mean_v = phase(k, now, jnp.concatenate([chl[k], gchl[k]], axis=0), total, optical, light)
            for f in range(4):
                mid[f, k] = now[f][0:tile]
            for side, offset, present in sides:
                @pl.when(present)
                def _():
                    mid_copy(k, side, offset, False).start()
            mix = 0.1 * now[2][0:tile] - 0.05 * now[3][0:tile]
            zero = jnp.zeros((tile, yt), jnp.float32)
            for sec in range(3):
                here = slice(sec * yt, (sec + 1) * yt)
                before = mean_v[:, (sec - 1) * yt:sec * yt] if sec > 0 else zero
                after = mean_v[:, (sec + 1) * yt:(sec + 2) * yt] if sec < 2 else zero
                drive_send[k, sec, 0] = mean_u[0:tile, here]
                drive_send[k, sec, 1] = mean_v[:, here]
                drive_send[k, sec, 2] = mix[:, here]
                drive_send[k, sec, 3] = jnp.where(lane_t == yt - 1, before, after)
                drive_row_send[k, sec, 0] = mean_u[wide - 1:wide, here]
                drive_row_send[k, sec, 1] = mean_u[tile:tile + 1, here]
            for sec in range(3):
                for copy in drive_copies(k, sec):
                    copy.start()

        @pl.loop(0, levels)
        def _(k):
            with scope("d_mid"):
                for side, offset, present in sides:
                    @pl.when(present)
                    def _():
                        mid_copy(k, side, offset, True).wait_recv()
            with scope("d_pig"):
                for sec in range(3):
                    pig_copy(k, sec, 0, strip).wait_recv()
                    for part, offset, present in ((1, 1, has_hi), (2, -1, has_lo)):
                        @pl.when(present)
                        def _():
                            pig_copy(k, sec, part, strip + offset).wait_recv()
            now = tuple(jnp.concatenate([mid[f, k], gmid[f, k]], axis=0) for f in range(4))
            pigment = jnp.concatenate([pig[sec, k] for sec in range(3)], axis=1)
            now, mean_u, mean_v = phase(k, now, pigment, total2, optical2, light2)
            items = (mean_u[0:tile], mean_v, now[2][0:tile], now[3][0:tile])
            for sec in range(3):
                for f in range(4):
                    drive2_send[k, sec, f] = items[f][:, sec * yt:(sec + 1) * yt]
            drive2_copy(k, 0).start()
            for f in range(4):
                flow_out[f, k] = now[f][0:tile]

        for sec in (1, 2):
            @pl.loop(0, levels)
            def _(k):
                drive2_copy(k, sec).start()

        with scope("d_light"):
            @pl.loop(0, levels)
            def _(k):
                for sec in range(3):
                    light_copy(k, jnp.int32(sec), sec * yt, strip).wait_recv()

        with scope("d_sends"):
            @pl.loop(0, levels)
            def _(k):
                for side, offset, present in sides:
                    @pl.when(present)
                    def _():
                        for copy in flow_copies(k, side, offset, False):
                            copy.wait_send()
                        mid_copy(k, side, offset, False).wait_send()
                for sec in range(3):
                    for copy in drive_copies(k, sec):
                        copy.wait_send()
                    drive2_copy(k, sec).wait_send()


    @pl.when(jnp.logical_not(is_dyn))
    def _():
        loads = [load(0, tracers_h, tracers), load(1, forcing_h, forcing), load(4, reaction_h, reaction)]
        begin = pl.multiple_of(strip * tile, tile)
        loads.extend((load(2, ocean_h.at[pl.ds(begin, tile), :], ocean.at[1]), load(3, bottom_h.at[pl.ds(begin, tile), :], bottom.at[1])))
        for copy in loads:
            copy.start()
        for _, offset, present in sides:
            @pl.when(present)
            def _():
                greet(barrier, section, strip + offset)
                greet(barrier, three, strip + offset)
        greet(barrier, three, strip)
        beside = ((0, -1, has_left), (1, 1, has_right))
        for _, offset, present in beside:
            @pl.when(present)
            def _():
                greet(barrier, section + offset, strip)
        for side, present, bufs in ((0, has_lo, (row_recv, row_recv2)), (1, has_hi, (row_recv, row_recv2)),
                                    (0, has_left, (col_recv, col_recv2)), (1, has_right, (col_recv, col_recv2))):
            @pl.when(jnp.logical_not(present))
            def _():
                for buf in bufs:
                    buf[side] = jnp.zeros(buf.shape[1:], jnp.float32)

        lane = lax.broadcasted_iota(jnp.int32, (tile, yt), 1)
        row = lax.broadcasted_iota(jnp.int32, (tile, yt), 0)
        pair = lax.div(lane, jnp.int32(2))
        odd = lax.rem(lane, jnp.int32(2)) == 1

        flow_out[...] = jnp.zeros_like(flow_out)
        light_out[...] = jnp.zeros_like(light_out)
        with scope('t_load'):
            for copy in loads:
                copy.wait()

        def pack(items):
            packed = jnp.zeros((tile, yt), jnp.float32)
            for i, x in enumerate(items):
                packed = jnp.where(pair == i, pltpu.roll(x, 2 * i + 1, 1), packed)
            return packed

        @pl.loop(0, levels)
        def _(k):
            items = [tracers[i, k] for i in range(nt)]
            col_send[k] = pack(items + [forcing[1, k]])
            for i, x in enumerate(items + [forcing[0, k]]):
                row_send[0, k, i] = x[0:1]
                row_send[1, k, i] = x[tile - 1:tile]

        left = pl.multiple_of(section * yt, yt)
        deep = jnp.where(ocean[1, :, pl.ds(left, yt)] == 1, bottom[1, :, pl.ds(left, yt)], 0)
        with scope('t_bar'):
            pl.semaphore_wait(barrier, lo_n + hi_n + has_left.astype(jnp.int32) + has_right.astype(jnp.int32))

        def row_copy(side, offset, arriving, s_buf, r_buf, ss, rs):
            at = side if arriving else 1 - side
            return remote(s_buf.at[side], r_buf.at[at], ss.at[side], rs.at[at], dev(section, strip + offset))

        def col_copy(side, offset, arriving, s_buf, r_buf, ss, rs):
            at = side if arriving else 1 - side
            return remote(s_buf, r_buf.at[at], ss.at[side], rs.at[at], dev(section + offset, strip))

        exchange_a = ((sides, row_copy, (row_send, row_recv, row_ss, row_rs)),
                      (beside, col_copy, (col_send, col_recv, col_ss, col_rs)))
        exchange_b = ((sides, row_copy, (row_send2, row_recv2, row2_ss, row2_rs)),
                      (beside, col_copy, (col_send2, col_recv2, col2_ss, col2_rs)))

        def run(exchange, arriving, what):
            for places, make, bufs in exchange:
                for side, offset, present in places:
                    @pl.when(present)
                    def _():
                        copy = make(side, offset, arriving, *bufs)
                        if what == "start":
                            copy.start()
                        elif what == "recv":
                            copy.wait_recv()
                        else:
                            copy.wait_send()

        run(exchange_a, False, "start")
        with scope('t_xa'):
            run(exchange_a, True, "recv")
        with scope('t_ready'):
            pl.semaphore_wait(ready, 1 + lo_n + hi_n)

        def tracer_step(k, cs, u, v, growth, u_lo, u_hi, v_edge, rows_of, packed):
            um, up, vm, vp = 1.0 - u, 1.0 + u, 1.0 - v, 1.0 + v
            hi_m, lo_p = 1.0 - u_hi, 1.0 + u_lo
            edge_m, edge_p = 1.0 - v_edge, 1.0 + v_edge
            wet = k < deep
            out = []
            for i in range(nt):
                c = cs[i]
                react = reaction[i, 0] * cs[0]
                for b in range(1, nt):
                    react = react + reaction[i, b] * cs[b]
                nxt = jnp.where(row == tile - 1, rows_of[1, k, i] * hi_m, pltpu.roll(c * um, tile - 1, 0))
                prv = jnp.where(row == 0, rows_of[0, k, i] * lo_p, pltpu.roll(c * up, 1, 0))
                edge = pltpu.roll(packed, yt - (2 * i + 1), 1)
                rgt = pltpu.roll(jnp.where(lane == 0, edge * edge_m, c * vm), yt - 1, 1)
                lft = pltpu.roll(jnp.where(lane == yt - 1, edge * edge_p, c * vp), 1, 1)
                out.append(jnp.where(wet, 0.8 * c + 0.05 * ((nxt + prv) + (rgt + lft)) + growth * react, 0.0))
            return out

        def pig_copies(k):
            return ((None, pig_copy(k, section, 0, strip)), (has_lo, pig_copy(k, section, 1, strip - 1)),
                    (has_hi, pig_copy(k, section, 2, strip + 1)))

        @pl.loop(0, levels)
        def _(k):
            cs = [tracers[i, k] for i in range(nt)]
            packed = jnp.where(odd, col_recv[1, k], col_recv[0, k])
            growth = 0.1 * jnp.exp(0.1 * forcing[2, k] - 0.05 * forcing[3, k])
            v_edge = pltpu.roll(packed, yt - (2 * nt + 1), 1)
            new = tracer_step(k, cs, forcing[0, k], forcing[1, k], growth, row_recv[0, k, nt], row_recv[1, k, nt], v_edge,
                              row_recv, packed)
            pigment = 0.25 * (new[0] * new[0] + new[1] * new[1])
            pig_s[k] = pigment
            for present, copy in pig_copies(k):
                if present is None:
                    copy.start()
                else:
                    pl.when(present)(copy.start)
            for i in range(nt):
                held[i, k] = new[i]
                row_send2[0, k, i] = new[i][0:1]
                row_send2[1, k, i] = new[i][tile - 1:tile]
            col_send2[k] = pack(new)

        run(exchange_b, False, "start")
        with scope('t_xb'):
            run(exchange_b, True, "recv")

        @pl.loop(0, levels)
        def _(k):
            origin = dev(three, strip)
            with scope("t_drive"):
                remote(drive_send.at[k, 0], drive.at[k], drive_ss.at[0, k], drive_rs.at[k], origin).wait_recv()
                remote(drive_row_send.at[k, 0], drive_row.at[k], drow_ss.at[0, k], drow_rs.at[k], origin).wait_recv()
            cs = [held[i, k] for i in range(nt)]
            packed = jnp.where(odd, col_recv2[1, k], col_recv2[0, k])
            growth = 0.1 * jnp.exp(drive[k, 2])
            new = tracer_step(k, cs, drive[k, 0], drive[k, 1], growth, drive_row[k, 0], drive_row[k, 1], drive[k, 3],
                              row_recv2, packed)
            light_s[k] = 0.25 * (new[0] * new[0] + new[1] * new[1])
            light_copy(k, section, left, strip).start()
            for i in range(nt):
                tracers_out[i, k] = new[i]

        @pl.loop(0, levels)
        def _(k):
            with scope("t_drive2"):
                remote(drive2_send.at[k, 0], forcing_out.at[:, k], drive2_ss.at[0, k], drive2_rs.at[k], dev(three, strip)).wait_recv()
            light_copy(k, section, left, strip).wait_send()
            for present, copy in pig_copies(k):
                if present is None:
                    copy.wait_send()
                else:
                    pl.when(present)(copy.wait_send)

        run(exchange_a, False, "send")
        run(exchange_b, False, "send")


def write_out(*refs):
    done = refs[-1]
    copies = [pltpu.make_async_copy(refs[i], refs[4 + i], done.at[i]) for i in range(4)]
    for copy in copies:
        copy.start()
    for copy in copies:
        copy.wait()


def solution(mesh):
    sizes = tuple(mesh.shape[a] for a in AXES)

    def on_device(flow, chl, tracers, forcing, ocean, bottom, reaction):
        levels, tile, cols = chl.shape
        nt, yt = tracers.shape[0], tracers.shape[3]
        f32 = jnp.float32

        def buf(*shape):
            return pltpu.VMEM(shape, f32)

        def sem(*shape):
            return pltpu.SemaphoreType.DMA(shape)

        wide = 2 * tile
        scratch = [
            buf(*flow.shape), buf(*chl.shape), buf(*tracers.shape), buf(*forcing.shape),
            pltpu.VMEM((3, tile, cols), jnp.int32), pltpu.VMEM((3, tile, cols), jnp.int32),
            pltpu.SMEM(reaction.shape, f32), sem(8),
            buf(*flow.shape), buf(*chl.shape), buf(*flow.shape), buf(*flow.shape), pltpu.VMEM((wide, cols), jnp.int32),
            buf(SUB, wide, cols), buf(wide, cols), buf(wide, cols),
            buf(SUB, wide, cols), buf(wide, cols), buf(wide, cols), buf(3, levels, wide, yt),
            buf(levels, 3, 4, tile, yt), buf(levels, 3, 2, 1, yt), buf(levels, 3, 4, tile, yt),
            buf(2, levels, nt + 1, 1, yt), buf(levels, tile, yt), buf(2, levels, nt + 1, 1, yt), buf(2, levels, tile, yt),
            buf(2, levels, nt, 1, yt), buf(levels, tile, yt), buf(2, levels, nt, 1, yt), buf(2, levels, tile, yt),
            buf(nt, levels, tile, yt), buf(levels, tile, yt),
            buf(levels, 4, tile, yt), buf(levels, 2, 1, yt), buf(levels, tile, yt),
            sem(2, levels), sem(2, levels), sem(2, levels), sem(2, levels), sem(2, levels), sem(2, levels),
            sem(2), sem(2), sem(2), sem(2),
            sem(2), sem(2), sem(2), sem(2),
            sem(3, levels), sem(3, 3, levels),
            sem(3, levels), sem(levels), sem(3, levels), sem(levels), sem(3, levels), sem(levels),
            sem(levels), sem(3, levels), pltpu.SemaphoreType.REGULAR,
        ]
        vmem = pl.BlockSpec(memory_space=pltpu.VMEM)
        shapes = [x.shape for x in (flow, chl, tracers, forcing)]
        room = 67043328 - 4 * sum(math.prod(x) for x in shapes) - 2**16
        results = pl.pallas_call(
            functools.partial(kernel, sizes),
            out_shape=[pltpu.VMEM(x, f32) for x in shapes],
            in_specs=[pl.BlockSpec(memory_space=pltpu.HBM)] * 7,
            out_specs=[vmem] * 4,
            scratch_shapes=scratch,
            compiler_params=pltpu.CompilerParams(collective_id=0, has_side_effects=True, vmem_limit_bytes=room),
        )(flow, chl, tracers, forcing, ocean, bottom, reaction)
        return pl.pallas_call(
            write_out,
            out_shape=[jax.ShapeDtypeStruct(x, f32) for x in shapes],
            in_specs=[vmem] * 4,
            out_specs=[pl.BlockSpec(memory_space=pltpu.HBM)] * 4,
            scratch_shapes=[sem(4)],
            compiler_params=pltpu.CompilerParams(vmem_limit_bytes=4 * 2**20),
        )(*results)

    rows4 = P(None, None, AXES, None)
    rows3 = P(None, AXES, None)
    return jax.shard_map(on_device, mesh=mesh, in_specs=(rows4, rows3, rows4, rows4, P(), P(), P()),
                         out_specs=(rows4, rows3, rows4, rows4), check_vma=False)
```

time: 29.6 us -> 27.2 us (0.919)
  the two profiles are of different devices: /device:TPU:1 before, /device:TPU:0 now
where the time goes in v1:
time: 27.2 us; the launch traced here: 27.1 us
  Pallas kernels  26.4 us (97%)
  between operations  0.64 us (2%)
    pallas_call x1, Pallas kernels, on_device(): pl.pallas_call(functools.partial(kernel, sizes), out_shape=[pltpu.VMEM(x,...  25.5 us
    pallas_call x1, Pallas kernels, on_device(): pl.pallas_call(write_out, out_shape=[jax.ShapeDtypeStruct(x, f32) for x i...  0.93 us

profile of v1, /device:TPU:0, one launch (start us, length us, event | category | flops | bytes accessed | tf_op | source)
XLA Modules:
  0.0 27.1 jit_solution(7918974942528321755)
XLA Ops:
  0.6 25.5 %shard_map.102 = (f32[4,6,8,384]{3,2,1,0:T(8,128)S(1)}, f32[6,8,384]{2,1,0:T(8,128)S(1)}, f32[16,6,8,128]{3,2,1,0:T(8,128)S(1)}, f32[4,6,8,128]{3,2,1,0:T(8,128)S(1)}) custom-call(f32[4,6,8,384]{3,2,1,0:T(8,128)} %flow_h.1, f32[6,8,384]{2,1,0:T(8,128)} %chl_h.1, f32[16,6,8,128]{3,2,1,0:T(8,128)} %tracers_h.1, f32[4,6,8,128]{3,2,1,0:T(8,128)} %forcing_h.1, ...), custom_call_target="tpu_custom_call" | custom-call | tf_op jit(solution)/shard_map/pallas_call | solution.py:500
  26.1 0.9 %shard_map.103 = (f32[4,6,8,384]{3,2,1,0:T(8,128)}, f32[6,8,384]{2,1,0:T(8,128)}, f32[16,6,8,128]{3,2,1,0:T(8,128)}, f32[4,6,8,128]{3,2,1,0:T(8,128)}) custom-call(f32[4,6,8,384]{3,2,1,0:T(8,128)S(1)} %get-tuple-element.8.refs_0_, f32[6,8,384]{2,1,0:T(8,128)S(1)} %get-tuple-element.9.refs_1_, f32[16,6,8,128]{3,2,1,0:T(8,128)S(1)} %get-tuple-element.10.refs_2_, ...), custom_call_target="tpu_custom_call" | custom-call | tf_op jit(solution)/shard_map/pallas_call | solution.py:508

commit v2 on v1

v2 whole, which is shorter than its diff:
```python
import functools
import math

import jax
import jax.numpy as jnp
from jax import lax
from jax.experimental import pallas as pl
from jax.experimental.pallas import tpu as pltpu
from jax.sharding import PartitionSpec as P

SUB = 4
MESH = pl.DeviceIdType.MESH
AXES = ("comp", "gy", "gx")


def substep(state, above, heat, wet, first, last):
    u, v, t, s = state
    rows, cols = u.shape
    p = above + 0.2 * (s - t)

    def row_next(x):
        return pltpu.roll(x, rows - 1, 0)

    def row_prev(x):
        return pltpu.roll(x, 1, 0)

    def col_next(x):
        return jnp.where(last, 0.0, pltpu.roll(x, cols - 1, 1))

    def col_prev(x):
        return jnp.where(first, 0.0, pltpu.roll(x, 1, 1))

    um, up, vm, vp = 1.0 - u, 1.0 + u, 1.0 - v, 1.0 + v
    new_u = 0.79 * u + 0.1 * v + 0.05 * (row_next(u - p) + row_prev(u + p) + col_next(u) + col_prev(u))
    new_v = 0.79 * v - 0.1 * u + 0.05 * (row_next(v) + row_prev(v) + col_next(v - p) + col_prev(v + p))
    new_t = 0.8 * t + 0.05 * (row_next(t * um) + row_prev(t * up) + col_next(t * vm) + col_prev(t * vp)) + heat
    new_s = 0.8 * s + 0.05 * (row_next(s * um) + row_prev(s * up) + col_next(s * vm) + col_prev(s * vp))
    return tuple(jnp.where(wet, x, 0.0) for x in (new_u, new_v, new_t, new_s)), p


D_HALO, D_MID, D_PIG = 0, 1, 2
T_DRIVE = 2
D_LIGHT, D_HALO_S, D_MID_S, D_DRIVE_S, D_DRIVE2_S, D_LOAD, D_MASK = range(7)
(T_ROW, T_COL, T_ROW2, T_COL2, T_ROW_S, T_ROW2_S, T_COL_S, T_COL2_S, T_PIG_S, T_SIDE_S, T_LIGHT_S, T_DRIVE2,
 T_LOAD, T_MASK, T_FORCE, T_REACT, T_HALO_S, T_MID_S) = (0, 1, 2, 3, 4, 5, 6, 8, 10, 11, 12, 13, 14, 15, 16, 17, 18, 19)
N_ONE = 20


def kernel(sizes, flow_h, chl_h, tracers_h, forcing_h, ocean_h, bottom_h, reaction_h,
           flow_out, light_out, tracers_out, forcing_out,
           flow, gflow, mid, gmid, masks, tracers, forcing, reaction, depth, total, optical, light, total2, optical2, light2, pig,
           drive_send, drive2_send, row_send, col_send, row_recv, col_recv, row_send2, col_send2, row_recv2, col_recv2,
           held, pig_s, drive, light_s, level_sem, one_sem, ready):
    n_comp, n_gy, n_gx = sizes
    grid = n_gy * n_gx
    every = n_comp * grid
    group = every // 4
    _, levels, tile, cols = mid.shape
    half = tile // 2
    wide = 2 * tile
    nt = tracers.shape[0]
    yt = tracers.shape[3]
    position = (lax.axis_index("comp") * grid + lax.axis_index("gy") * n_gx + lax.axis_index("gx")).astype(jnp.int32)
    moved = lax.rem(position + 1, jnp.int32(every))
    strip = lax.rem(moved, jnp.int32(group))
    section = lax.div(moved, jnp.int32(group))
    is_dyn = section == 3
    has_lo = strip > 0
    has_hi = strip < group - 1
    has_left = section > 0
    has_right = section < 2

    def dev(sec, row):
        pos = lax.rem(sec * group + row + (every - 1), jnp.int32(every))
        return (lax.div(pos, jnp.int32(grid)), lax.rem(lax.div(pos, jnp.int32(n_gx)), jnp.int32(n_gy)),
                lax.rem(pos, jnp.int32(n_gx)))

    def remote(src, dst, send_sem, recv_sem, target):
        return pltpu.make_async_remote_copy(src_ref=src, dst_ref=dst, send_sem=send_sem, recv_sem=recv_sem,
                                            device_id=target, device_id_type=MESH)

    three = jnp.int32(3)
    scope = jax.named_scope
    barrier = pltpu.get_barrier_semaphore()

    def load(i, src, dst):
        return pltpu.make_async_copy(src, dst, one_sem.at[i])

    def mask_loads(sem, part, offset):
        begin = pl.multiple_of(jnp.clip(strip + offset, 0, group - 1) * tile, tile)
        return [load(sem, h.at[pl.ds(begin, tile), :], masks.at[part, m]) for m, h in enumerate((ocean_h, bottom_h))]

    def greet(sem, sec, row):
        pl.semaphore_signal(sem, inc=1, device_id=dev(sec, row), device_id_type=MESH)

    sides = ((0, -1, has_lo), (1, 1, has_hi))
    lo_n = has_lo.astype(jnp.int32)
    hi_n = has_hi.astype(jnp.int32)

    both = has_lo & has_hi
    rows_drive = 3 * tile + 2

    def for_sides(act):
        pl.when(both)(lambda: act(True))
        pl.when(jnp.logical_not(both))(lambda: act(False))

    def pig_copy(k, sec, part, row):
        from_rows = (pl.ds(0, tile), pl.ds(0, half), pl.ds(half, half))[part]
        to_rows = (pl.ds(0, tile), pl.ds(tile, half), pl.ds(tile + half, half))[part]
        return remote(pig_s.at[k, from_rows], pig.at[sec, k, to_rows], one_sem.at[T_PIG_S if part == 0 else T_SIDE_S],
                      level_sem.at[D_PIG, k], dev(three, row))

    def light_copy(k, sec, begin, row):
        return remote(light_s.at[k], light_out.at[k, :, pl.ds(begin, yt)], one_sem.at[T_LIGHT_S], one_sem.at[D_LIGHT],
                      dev(three, row))

    other = dev(lax.rem(section + 1, jnp.int32(4)), strip)

    def recv(dst, sem):
        remote(dst, dst, sem, sem, other).wait_recv()

    def sent(src, sem):
        remote(src, src, sem, sem, other).wait_send()

    halo_of = ((flow, gflow, D_HALO_S, D_HALO), (mid, gmid, D_MID_S, D_MID))

    def halo_copy(what, k, side, offset):
        own, ghost, send, come = halo_of[what]
        place = pl.ds(half * side, half)
        to = strip + offset
        where = dev(three * jnp.minimum(to, 1), to)
        return remote(own.at[:, k, place, :], ghost.at[:, k, place, :], one_sem.at[send], level_sem.at[come, k], where)

    def relay_copy(what, k):
        _, ghost, _, come = halo_of[what]
        place = pl.ds(0, half)
        return remote(ghost.at[:, k, place, :], ghost.at[:, k, place, :], one_sem.at[(T_HALO_S, T_MID_S)[what]],
                      level_sem.at[come, k], dev(three, strip))

    @pl.when(is_dyn)
    def _():
        loads = [load(D_LOAD, flow_h, flow.at[0:4]), load(D_LOAD, chl_h, flow.at[4])]
        for part in range(3):
            loads.extend(mask_loads(D_MASK, part, part - 1))
        for copy in loads:
            copy.start()
        for _, offset, present in sides:
            @pl.when(present)
            def _():
                greet(barrier, three, strip + offset)
        for place, present in ((half, has_lo), (0, has_hi)):
            @pl.when(jnp.logical_not(present))
            def _():
                for f in range(5):
                    gflow[f, :, place:place + half, :] = jnp.zeros((levels, half, cols), jnp.float32)
                for f in range(4):
                    gmid[f, :, place:place + half, :] = jnp.zeros((levels, half, cols), jnp.float32)
                for sec in range(3):
                    pig[sec, :, tile + place:tile + place + half, :] = jnp.zeros((levels, half, yt), jnp.float32)
        total[...] = jnp.zeros_like(total)
        total2[...] = jnp.zeros_like(total2)
        optical[...] = jnp.zeros_like(optical)
        optical2[...] = jnp.zeros_like(optical2)
        light[...] = jnp.ones_like(light)
        light2[...] = jnp.ones_like(light2)
        with scope("d_load"):
            load(D_LOAD, flow, flow).wait()
            load(D_MASK, masks, masks).wait()
        with scope("d_bar"):
            pl.semaphore_wait(barrier, 3 + 4 * lo_n + 4 * hi_n)

        def drive_copy(k, sec):
            return remote(drive_send.at[k, sec, pl.ds(0, rows_drive)], drive.at[k, pl.ds(0, rows_drive)],
                          one_sem.at[D_DRIVE_S], level_sem.at[T_DRIVE, k], dev(jnp.int32(sec), strip))

        def edge_copy(k, sec, side, offset):
            return remote(drive_send.at[k, sec, pl.ds(side * (tile - 1), 1)], drive.at[k, pl.ds(rows_drive + 1 - side, 1)],
                          one_sem.at[D_DRIVE_S], level_sem.at[T_DRIVE, k], dev(jnp.int32(sec), strip + offset))

        def drive2_copy(k, sec):
            return remote(drive2_send.at[k, sec], forcing_out.at[:, k], one_sem.at[D_DRIVE2_S], one_sem.at[T_DRIVE2],
                          dev(jnp.int32(sec), strip))

        @pl.loop(0, levels)
        def _(k):
            for side, offset, present in sides:
                @pl.when(present)
                def _():
                    halo_copy(0, k, side, offset).start()

        for sec in range(3):
            greet(ready, jnp.int32(sec), strip)
            for _, offset, present in sides:
                @pl.when(present)
                def _():
                    greet(ready, jnp.int32(sec), strip + offset)

        def deep_of(part):
            return jnp.where(masks[part, 0] == 1, masks[part, 1], 0)

        row_d = lax.broadcasted_iota(jnp.int32, (tile, cols), 0)
        depth[0:tile, :] = deep_of(1)
        depth[tile:wide, :] = jnp.where(row_d < half, deep_of(2) * hi_n, deep_of(0) * lo_n)
        tracers_out[...] = jnp.zeros_like(tracers_out)
        forcing_out[...] = jnp.zeros_like(forcing_out)

        on_diagonal = lax.broadcasted_iota(jnp.int32, (tile, yt), 0) == lax.broadcasted_iota(jnp.int32, (tile, yt), 1)
        lane_d = lax.broadcasted_iota(jnp.int32, (wide, cols), 1)

        def phase(k, now, pigment, sums, opt_s, light_ref):
            first, last = lane_d == 0, lane_d == cols - 1
            opt = opt_s[...] + (0.05 + 0.3 * pigment)
            lower = jnp.exp(-opt)
            heat = 0.5 * (light_ref[...] - lower)
            opt_s[...] = opt
            light_ref[...] = lower
            wet = k < depth[...]
            sum_u = None
            for n in range(SUB):
                now, p = substep(now, sums[n], heat, wet, first, last)
                sums[n] = p
                sum_u = now[0] if n == 0 else sum_u + now[0]
                sum_v = now[1] if n == 0 else sum_v + now[1]
            return now, sum_u * (1.0 / SUB), sum_v[0:tile] * (1.0 / SUB)

        @pl.loop(0, levels)
        def _(k):
            with scope("d_halo"):
                for_sides(lambda two: recv(gflow.at[:, k, pl.ds(0, tile if two else half), :], level_sem.at[D_HALO, k]))
            now = tuple(jnp.concatenate([flow[f, k], gflow[f, k]], axis=0) for f in range(4))
            now, mean_u, mean_v = phase(k, now, jnp.concatenate([flow[4, k], gflow[4, k]], axis=0), total, optical, light)
            for f in range(4):
                mid[f, k] = now[f][0:tile]
            for side, offset, present in sides:
                @pl.when(present)
                def _():
                    halo_copy(1, k, side, offset).start()
            mix = 0.1 * now[2][0:tile] - 0.05 * now[3][0:tile]
            for sec in range(3):
                here = slice(sec * yt, (sec + 1) * yt)
                drive_send[k, sec, 0:tile] = mean_u[0:tile, here]
                drive_send[k, sec, tile:2 * tile] = mean_v[:, here]
                drive_send[k, sec, 2 * tile:3 * tile] = mix[:, here]
                for at, edge, inside in ((0, sec * yt - 1, sec > 0), (1, (sec + 1) * yt, sec < 2)):
                    if inside:
                        spread = jnp.where(on_diagonal, mean_v[:, edge:edge + 1], 0.0)
                        drive_send[k, sec, 3 * tile + at:3 * tile + at + 1] = jnp.sum(spread, axis=0, keepdims=True)
                    else:
                        drive_send[k, sec, 3 * tile + at:3 * tile + at + 1] = jnp.zeros((1, yt), jnp.float32)
            for sec in range(3):
                drive_copy(k, sec).start()
            for side, offset, present in sides:
                @pl.when(present)
                def _():
                    for sec in range(3):
                        edge_copy(k, sec, side, offset).start()

        @pl.loop(0, levels)
        def _(k):
            with scope("d_mid"):
                for_sides(lambda two: recv(gmid.at[:, k, pl.ds(0, tile if two else half), :], level_sem.at[D_MID, k]))
            with scope("d_pig"):
                for_sides(lambda two: recv(pig.at[:, k, pl.ds(0, wide if two else tile + half), :], level_sem.at[D_PIG, k]))
            now = tuple(jnp.concatenate([mid[f, k], gmid[f, k]], axis=0) for f in range(4))
            pigment = jnp.concatenate([pig[sec, k] for sec in range(3)], axis=1)
            now, mean_u, mean_v = phase(k, now, pigment, total2, optical2, light2)
            items = (mean_u[0:tile], mean_v, now[2][0:tile], now[3][0:tile])
            for sec in range(3):
                for f in range(4):
                    drive2_send[k, sec, f] = items[f][:, sec * yt:(sec + 1) * yt]
            drive2_copy(k, 0).start()
            for f in range(4):
                flow_out[f, k] = now[f][0:tile]

        for sec in (1, 2):
            @pl.loop(0, levels)
            def _(k):
                drive2_copy(k, sec).start()

        with scope("d_light"):
            recv(light_out, one_sem.at[D_LIGHT])
        with scope("d_sends"):
            for_sides(lambda two: sent(flow.at[:, :, pl.ds(0, tile if two else half), :], one_sem.at[D_HALO_S]))
            for_sides(lambda two: sent(mid.at[:, :, pl.ds(0, tile if two else half), :], one_sem.at[D_MID_S]))
            for_sides(lambda two: sent(drive_send.at[:, :, pl.ds(0, rows_drive + (2 if two else 1)), :], one_sem.at[D_DRIVE_S]))
            sent(drive2_send, one_sem.at[D_DRIVE2_S])

    @pl.when(jnp.logical_not(is_dyn))
    def _():
        loads = [load(T_LOAD, tracers_h, tracers), load(T_FORCE, forcing_h, forcing), load(T_REACT, reaction_h, reaction)]
        loads.extend(mask_loads(T_MASK, 1, 0))
        for copy in loads:
            copy.start()
        for _, offset, present in sides:
            @pl.when(present)
            def _():
                greet(barrier, section, strip + offset)
                greet(barrier, three, strip + offset)
        greet(barrier, three, strip)
        beside = ((0, -1, has_left), (1, 1, has_right))
        for _, offset, present in beside:
            @pl.when(present)
            def _():
                greet(barrier, section + offset, strip)
        for side, present in ((0, has_lo), (1, has_hi)):
            @pl.when(jnp.logical_not(present))
            def _():
                drive[:, rows_drive + side:rows_drive + side + 1] = jnp.zeros((levels, 1, yt), jnp.float32)
        for side, present, bufs in ((0, has_lo, (row_recv, row_recv2)), (1, has_hi, (row_recv, row_recv2)),
                                    (0, has_left, (col_recv, col_recv2)), (1, has_right, (col_recv, col_recv2))):
            @pl.when(jnp.logical_not(present))
            def _():
                for buf in bufs:
                    buf[side] = jnp.zeros(buf.shape[1:], jnp.float32)

        lane = lax.broadcasted_iota(jnp.int32, (tile, yt), 1)
        row = lax.broadcasted_iota(jnp.int32, (tile, yt), 0)
        pair = lax.div(lane, jnp.int32(2))
        odd = lax.rem(lane, jnp.int32(2)) == 1
        relays = (section == 0) & (strip == 0)

        flow_out[...] = jnp.zeros_like(flow_out)
        light_out[...] = jnp.zeros_like(light_out)
        with scope('t_load'):
            for copy in loads[:3]:
                copy.wait()
            load(T_MASK, masks.at[1], masks.at[1]).wait()

        def pack(items):
            packed = jnp.zeros((tile, yt), jnp.float32)
            for i, x in enumerate(items):
                packed = jnp.where(pair == i, pltpu.roll(x, 2 * i + 1, 1), packed)
            return packed

        @pl.loop(0, levels)
        def _(k):
            items = [tracers[i, k] for i in range(nt)]
            col_send[k] = pack(items + [forcing[1, k]])
            for i, x in enumerate(items + [forcing[0, k]]):
                row_send[0, k, i] = x[0:1]
                row_send[1, k, i] = x[tile - 1:tile]

        left = pl.multiple_of(section * yt, yt)
        deep = jnp.where(masks[1, 0, :, pl.ds(left, yt)] == 1, masks[1, 1, :, pl.ds(left, yt)], 0)
        with scope('t_bar'):
            pl.semaphore_wait(barrier, lo_n + hi_n + has_left.astype(jnp.int32) + has_right.astype(jnp.int32))

        def row_copies(s_buf, r_buf, ss, rs):
            return [(present, remote(s_buf.at[side], r_buf.at[1 - side], one_sem.at[ss], one_sem.at[rs], dev(section, strip + offset)))
                    for side, offset, present in sides]

        def col_copies(s_buf, r_buf, ss, rs):
            return [(present, remote(s_buf, r_buf.at[1 - side], one_sem.at[ss + side], one_sem.at[rs], dev(section + offset, strip)))
                    for side, offset, present in beside]

        exchange_a = ((row_send, row_recv, T_ROW_S, T_ROW), (col_send, col_recv, T_COL_S, T_COL))
        exchange_b = ((row_send2, row_recv2, T_ROW2_S, T_ROW2), (col_send2, col_recv2, T_COL2_S, T_COL2))

        def start(exchange):
            for present, copy in row_copies(*exchange[0]) + col_copies(*exchange[1]):
                pl.when(present)(copy.start)

        def arrive(exchange):
            (_, rows, _, rs), (_, ends, _, cs) = exchange
            for_sides(lambda two: recv(rows if two else rows.at[0], one_sem.at[rs]))
            middle = has_left & has_right
            pl.when(middle)(lambda: recv(ends, one_sem.at[cs]))
            pl.when(jnp.logical_not(middle))(lambda: recv(ends.at[0], one_sem.at[cs]))

        def finish(exchange):
            for_sides(lambda two: sent(exchange[0][0] if two else exchange[0][0].at[0], one_sem.at[exchange[0][2]]))
            for present, copy in col_copies(*exchange[1]):
                pl.when(present)(copy.wait_send)

        def relay(what):
            @pl.when(relays)
            def _():
                @pl.loop(0, levels)
                def _(k):
                    recv(halo_of[what][1].at[:, k, pl.ds(0, half), :], level_sem.at[halo_of[what][3], k])
                    relay_copy(what, k).start()

        with scope("t_ready"):
            start(exchange_a)
            pl.semaphore_wait(ready, 1 + lo_n + hi_n)
        with scope("t_relay"):
            relay(0)
        with scope("t_xa"):
            arrive(exchange_a)

        def tracer_step(k, cs, u, v, growth, u_lo, u_hi, v_edge, rows_of, packed):
            um, up, vm, vp = 1.0 - u, 1.0 + u, 1.0 - v, 1.0 + v
            hi_m, lo_p = 1.0 - u_hi, 1.0 + u_lo
            edge_m, edge_p = 1.0 - v_edge, 1.0 + v_edge
            wet = k < deep
            out = []
            for i in range(nt):
                c = cs[i]
                react = reaction[i, 0] * cs[0]
                for b in range(1, nt):
                    react = react + reaction[i, b] * cs[b]
                nxt = jnp.where(row == tile - 1, rows_of[1, k, i] * hi_m, pltpu.roll(c * um, tile - 1, 0))
                prv = jnp.where(row == 0, rows_of[0, k, i] * lo_p, pltpu.roll(c * up, 1, 0))
                edge = pltpu.roll(packed, yt - (2 * i + 1), 1)
                rgt = pltpu.roll(jnp.where(lane == 0, edge * edge_m, c * vm), yt - 1, 1)
                lft = pltpu.roll(jnp.where(lane == yt - 1, edge * edge_p, c * vp), 1, 1)
                out.append(jnp.where(wet, 0.8 * c + 0.05 * ((nxt + prv) + (rgt + lft)) + growth * react, 0.0))
            return out

        def pig_copies(k):
            return ((None, pig_copy(k, section, 0, strip)), (has_lo, pig_copy(k, section, 1, strip - 1)),
                    (has_hi, pig_copy(k, section, 2, strip + 1)))

        @pl.loop(0, levels)
        def _(k):
            cs = [tracers[i, k] for i in range(nt)]
            packed = jnp.where(odd, col_recv[1, k], col_recv[0, k])
            growth = 0.1 * jnp.exp(0.1 * forcing[2, k] - 0.05 * forcing[3, k])
            v_edge = pltpu.roll(packed, yt - (2 * nt + 1), 1)
            new = tracer_step(k, cs, forcing[0, k], forcing[1, k], growth, row_recv[0, k, nt], row_recv[1, k, nt], v_edge,
                              row_recv, packed)
            pigment = 0.25 * (new[0] * new[0] + new[1] * new[1])
            pig_s[k] = pigment
            for present, copy in pig_copies(k):
                if present is None:
                    copy.start()
                else:
                    pl.when(present)(copy.start)
            for i in range(nt):
                held[i, k] = new[i]
                row_send2[0, k, i] = new[i][0:1]
                row_send2[1, k, i] = new[i][tile - 1:tile]
            col_send2[k] = pack(new)

        start(exchange_b)
        with scope("t_relay2"):
            relay(1)
        with scope('t_xb'):
            arrive(exchange_b)

        @pl.loop(0, levels)
        def _(k):
            with scope("t_drive"):
                for_sides(lambda two: recv(drive.at[k, pl.ds(0, rows_drive + (2 if two else 1))], level_sem.at[T_DRIVE, k]))
            cs = [held[i, k] for i in range(nt)]
            packed = jnp.where(odd, col_recv2[1, k], col_recv2[0, k])
            growth = 0.1 * jnp.exp(drive[k, 2 * tile:3 * tile])
            ends = [jnp.sum(jnp.where(lane == row, drive[k, 3 * tile + at:3 * tile + at + 1], 0.0), axis=1, keepdims=True)
                    for at in range(2)]
            v_edge = jnp.where(lane == 0, ends[1], ends[0])
            new = tracer_step(k, cs, drive[k, 0:tile], drive[k, tile:2 * tile], growth, drive[k, rows_drive:rows_drive + 1],
                              drive[k, rows_drive + 1:rows_drive + 2], v_edge, row_recv2, packed)
            light_s[k] = 0.25 * (new[0] * new[0] + new[1] * new[1])
            light_copy(k, section, left, strip).start()
            for i in range(nt):
                tracers_out[i, k] = new[i]

        with scope("t_drive2"):
            recv(forcing_out, one_sem.at[T_DRIVE2])
        sent(light_s, one_sem.at[T_LIGHT_S])
        sent(pig_s, one_sem.at[T_PIG_S])
        for_sides(lambda two: sent(pig_s if two else pig_s.at[:, pl.ds(0, half)], one_sem.at[T_SIDE_S]))
        finish(exchange_a)
        finish(exchange_b)

        @pl.when(relays)
        def _():
            for what in range(2):
                sent(halo_of[what][1].at[:, :, pl.ds(0, half), :], one_sem.at[(T_HALO_S, T_MID_S)[what]])


def write_out(*refs):
    done = refs[-1]
    copies = [pltpu.make_async_copy(refs[i], refs[4 + i], done.at[i]) for i in range(4)]
    for copy in copies:
        copy.start()
    for copy in copies:
        copy.wait()


def solution(mesh):
    sizes = tuple(mesh.shape[a] for a in AXES)

    def on_device(flow, chl, tracers, forcing, ocean, bottom, reaction):
        levels, tile, cols = chl.shape
        nt, yt = tracers.shape[0], tracers.shape[3]
        f32 = jnp.float32

        def buf(*shape):
            return pltpu.VMEM(shape, f32)

        def sem(*shape):
            return pltpu.SemaphoreType.DMA(shape)

        wide = 2 * tile
        scratch = [
            buf(5, levels, tile, cols), buf(5, levels, tile, cols), buf(*flow.shape), buf(*flow.shape),
            pltpu.VMEM((3, 2, tile, cols), jnp.int32), buf(*tracers.shape), buf(*forcing.shape), pltpu.SMEM(reaction.shape, f32),
            pltpu.VMEM((wide, cols), jnp.int32), buf(SUB, wide, cols), buf(wide, cols), buf(wide, cols),
            buf(SUB, wide, cols), buf(wide, cols), buf(wide, cols), buf(3, levels, wide, yt),
            buf(levels, 3, 4 * tile, yt), buf(levels, 3, 4, tile, yt),
            buf(2, levels, nt + 1, 1, yt), buf(levels, tile, yt), buf(2, levels, nt + 1, 1, yt), buf(2, levels, tile, yt),
            buf(2, levels, nt, 1, yt), buf(levels, tile, yt), buf(2, levels, nt, 1, yt), buf(2, levels, tile, yt),
            buf(nt, levels, tile, yt), buf(levels, tile, yt),
            buf(levels, 4 * tile, yt), buf(levels, tile, yt),
            sem(3, levels), sem(N_ONE), pltpu.SemaphoreType.REGULAR,
        ]
        vmem = pl.BlockSpec(memory_space=pltpu.VMEM)
        shapes = [x.shape for x in (flow, chl, tracers, forcing)]
        room = 67043328 - 4 * sum(math.prod(x) for x in shapes) - 2**16
        results = pl.pallas_call(
            functools.partial(kernel, sizes),
            out_shape=[pltpu.VMEM(x, f32) for x in shapes],
            in_specs=[pl.BlockSpec(memory_space=pltpu.HBM)] * 7,
            out_specs=[vmem] * 4,
            scratch_shapes=scratch,
            compiler_params=pltpu.CompilerParams(collective_id=0, has_side_effects=True, vmem_limit_bytes=room),
        )(flow, chl, tracers, forcing, ocean, bottom, reaction)
        return pl.pallas_call(
            write_out,
            out_shape=[jax.ShapeDtypeStruct(x, f32) for x in shapes],
            in_specs=[vmem] * 4,
            out_specs=[pl.BlockSpec(memory_space=pltpu.HBM)] * 4,
            scratch_shapes=[sem(4)],
            compiler_params=pltpu.CompilerParams(vmem_limit_bytes=4 * 2**20),
        )(*results)

    rows4 = P(None, None, AXES, None)
    rows3 = P(None, AXES, None)
    return jax.shard_map(on_device, mesh=mesh, in_specs=(rows4, rows3, rows4, rows4, P(), P(), P()),
                         out_specs=(rows4, rows3, rows4, rows4), check_vma=False)
```

time: 27.2 us -> 23.7 us (0.87)
  Pallas kernels: 26.4 us -> 22.9 us
    pallas_call x1, Pallas kernels: 25.5 us -> 21.9 us  [on_device(): pl.pallas_call(functools.partial(kernel, sizes), out_shape=[pltpu.VMEM(x,...]
where the time goes in v2:
time: 23.7 us; the launch traced here: 23.5 us
  Pallas kernels  22.9 us (97%)
  between operations  0.64 us (3%)
    pallas_call x1, Pallas kernels, on_device(): pl.pallas_call(functools.partial(kernel, sizes), out_shape=[pltpu.VMEM(x,...  21.9 us
    pallas_call x1, Pallas kernels, on_device(): pl.pallas_call(write_out, out_shape=[jax.ShapeDtypeStruct(x, f32) for x i...  0.93 us

profile of v2, /device:TPU:0, one launch (start us, length us, event | category | flops | bytes accessed | tf_op | source)
XLA Modules:
  0.0 23.5 jit_solution(17399463399330851893)
XLA Ops:
  0.6 21.9 %shard_map.102 = (f32[4,6,8,384]{3,2,1,0:T(8,128)S(1)}, f32[6,8,384]{2,1,0:T(8,128)S(1)}, f32[16,6,8,128]{3,2,1,0:T(8,128)S(1)}, f32[4,6,8,128]{3,2,1,0:T(8,128)S(1)}) custom-call(f32[4,6,8,384]{3,2,1,0:T(8,128)} %flow_h.1, f32[6,8,384]{2,1,0:T(8,128)} %chl_h.1, f32[16,6,8,128]{3,2,1,0:T(8,128)} %tracers_h.1, f32[4,6,8,128]{3,2,1,0:T(8,128)} %forcing_h.1, ...), custom_call_target="tpu_custom_call" | custom-call | tf_op jit(solution)/shard_map/pallas_call | solution.py:511
  22.6 0.9 %shard_map.103 = (f32[4,6,8,384]{3,2,1,0:T(8,128)}, f32[6,8,384]{2,1,0:T(8,128)}, f32[16,6,8,128]{3,2,1,0:T(8,128)}, f32[4,6,8,128]{3,2,1,0:T(8,128)}) custom-call(f32[4,6,8,384]{3,2,1,0:T(8,128)S(1)} %get-tuple-element.8.refs_0_, f32[6,8,384]{2,1,0:T(8,128)S(1)} %get-tuple-element.9.refs_1_, f32[16,6,8,128]{3,2,1,0:T(8,128)S(1)} %get-tuple-element.10.refs_2_, ...), custom_call_target="tpu_custom_call" | custom-call | tf_op jit(solution)/shard_map/pallas_call | solution.py:519

commit v3 on v2

--- a/solution.py
+++ b/solution.py
@@ -13,7 +13,7 @@
 AXES = ("comp", "gy", "gx")
 
 
-def substep(state, above, heat, wet, first, last):
+def substep(state, above, heat, wet, first, last, lanes):
     u, v, t, s = state
     rows, cols = u.shape
     p = above + 0.2 * (s - t)
@@ -24,11 +24,16 @@
     def row_prev(x):
         return pltpu.roll(x, 1, 0)
 
+    def col_shift(x, shift, at_edge, step):
+        turned = [pltpu.roll(x[:, a:a + lanes], shift, 1) for a in range(0, cols, lanes)]
+        beside = [turned[i + step] if 0 <= i + step < len(turned) else 0.0 for i in range(len(turned))]
+        return jnp.concatenate([jnp.where(at_edge, b, x) for x, b in zip(turned, beside)], axis=1)
+
     def col_next(x):
-        return jnp.where(last, 0.0, pltpu.roll(x, cols - 1, 1))
+        return col_shift(x, lanes - 1, last, 1)
 
     def col_prev(x):
-        return jnp.where(first, 0.0, pltpu.roll(x, 1, 1))
+        return col_shift(x, 1, first, -1)
 
     um, up, vm, vp = 1.0 - u, 1.0 + u, 1.0 - v, 1.0 + v
     new_u = 0.79 * u + 0.1 * v + 0.05 * (row_next(u - p) + row_prev(u + p) + col_next(u) + col_prev(u))
@@ -39,11 +44,11 @@
 
 
 D_HALO, D_MID, D_PIG = 0, 1, 2
-T_DRIVE = 2
+T_DRIVE, T_ROW2, T_COL2 = 2, 3, 4
 D_LIGHT, D_HALO_S, D_MID_S, D_DRIVE_S, D_DRIVE2_S, D_LOAD, D_MASK = range(7)
-(T_ROW, T_COL, T_ROW2, T_COL2, T_ROW_S, T_ROW2_S, T_COL_S, T_COL2_S, T_PIG_S, T_SIDE_S, T_LIGHT_S, T_DRIVE2,
- T_LOAD, T_MASK, T_FORCE, T_REACT, T_HALO_S, T_MID_S) = (0, 1, 2, 3, 4, 5, 6, 8, 10, 11, 12, 13, 14, 15, 16, 17, 18, 19)
-N_ONE = 20
+(T_ROW, T_COL, T_ROW_S, T_ROW2_S, T_COL_S, T_COL2_S, T_PIG_S, T_SIDE_S, T_LIGHT_S, T_DRIVE2,
+ T_LOAD, T_MASK, T_FORCE, T_REACT, T_MID_S) = (0, 1, 2, 3, 4, 6, 8, 9, 10, 11, 12, 13, 14, 15, 16)
+N_ONE = 17
 
 
 def kernel(sizes, flow_h, chl_h, tracers_h, forcing_h, ocean_h, bottom_h, reaction_h,
@@ -128,14 +133,13 @@
         own, ghost, send, come = halo_of[what]
         place = pl.ds(half * side, half)
         to = strip + offset
-        where = dev(three * jnp.minimum(to, 1), to)
+        where = dev(three * jnp.minimum(to, 1) if what == 1 else three, to)
         return remote(own.at[:, k, place, :], ghost.at[:, k, place, :], one_sem.at[send], level_sem.at[come, k], where)
 
-    def relay_copy(what, k):
-        _, ghost, _, come = halo_of[what]
+    def relay_copy(k):
         place = pl.ds(0, half)
-        return remote(ghost.at[:, k, place, :], ghost.at[:, k, place, :], one_sem.at[(T_HALO_S, T_MID_S)[what]],
-                      level_sem.at[come, k], dev(three, strip))
+        return remote(gmid.at[:, k, place, :], gmid.at[:, k, place, :], one_sem.at[T_MID_S], level_sem.at[D_MID, k],
+                      dev(three, strip))
 
     @pl.when(is_dyn)
     def _():
@@ -205,10 +209,10 @@
         forcing_out[...] = jnp.zeros_like(forcing_out)
 
         on_diagonal = lax.broadcasted_iota(jnp.int32, (tile, yt), 0) == lax.broadcasted_iota(jnp.int32, (tile, yt), 1)
-        lane_d = lax.broadcasted_iota(jnp.int32, (wide, cols), 1)
+        lane_d = lax.broadcasted_iota(jnp.int32, (wide, yt), 1)
 
         def phase(k, now, pigment, sums, opt_s, light_ref):
-            first, last = lane_d == 0, lane_d == cols - 1
+            first, last = lane_d == 0, lane_d == yt - 1
             opt = opt_s[...] + (0.05 + 0.3 * pigment)
             lower = jnp.exp(-opt)
             heat = 0.5 * (light_ref[...] - lower)
@@ -217,7 +221,7 @@
             wet = k < depth[...]
             sum_u = None
             for n in range(SUB):
-                now, p = substep(now, sums[n], heat, wet, first, last)
+                now, p = substep(now, sums[n], heat, wet, first, last, yt)
                 sums[n] = p
                 sum_u = now[0] if n == 0 else sum_u + now[0]
                 sum_v = now[1] if n == 0 else sum_v + now[1]
@@ -345,48 +349,39 @@
         with scope('t_bar'):
             pl.semaphore_wait(barrier, lo_n + hi_n + has_left.astype(jnp.int32) + has_right.astype(jnp.int32))
 
-        def row_copies(s_buf, r_buf, ss, rs):
-            return [(present, remote(s_buf.at[side], r_buf.at[1 - side], one_sem.at[ss], one_sem.at[rs], dev(section, strip + offset)))
-                    for side, offset, present in sides]
-
-        def col_copies(s_buf, r_buf, ss, rs):
-            return [(present, remote(s_buf, r_buf.at[1 - side], one_sem.at[ss + side], one_sem.at[rs], dev(section + offset, strip)))
-                    for side, offset, present in beside]
-
-        exchange_a = ((row_send, row_recv, T_ROW_S, T_ROW), (col_send, col_recv, T_COL_S, T_COL))
-        exchange_b = ((row_send2, row_recv2, T_ROW2_S, T_ROW2), (col_send2, col_recv2, T_COL2_S, T_COL2))
+        def copies(rows_s, rows_r, cols_s, cols_r, row_ss, row_rs, col_ss, col_rs):
+            for side, offset, present in sides:
+                yield present, remote(rows_s.at[side], rows_r.at[1 - side], one_sem.at[row_ss], row_rs, dev(section, strip + offset))
+            for side, offset, present in beside:
+                yield present, remote(cols_s, cols_r.at[1 - side], one_sem.at[col_ss + side], col_rs, dev(section + offset, strip))
+
+        def exchange_a():
+            return copies(row_send, row_recv, col_send, col_recv, T_ROW_S, one_sem.at[T_ROW], T_COL_S, one_sem.at[T_COL])
+
+        def exchange_b(k):
+            return copies(row_send2.at[:, k], row_recv2.at[:, k], col_send2.at[k], col_recv2.at[:, k],
+                          T_ROW2_S, level_sem.at[T_ROW2, k], T_COL2_S, level_sem.at[T_COL2, k])
 
         def start(exchange):
-            for present, copy in row_copies(*exchange[0]) + col_copies(*exchange[1]):
+            for present, copy in exchange:
                 pl.when(present)(copy.start)
 
-        def arrive(exchange):
-            (_, rows, _, rs), (_, ends, _, cs) = exchange
-            for_sides(lambda two: recv(rows if two else rows.at[0], one_sem.at[rs]))
+        def arrive(rows_r, cols_r, row_rs, col_rs):
+            for_sides(lambda two: recv(rows_r if two else rows_r.at[0], row_rs))
             middle = has_left & has_right
-            pl.when(middle)(lambda: recv(ends, one_sem.at[cs]))
-            pl.when(jnp.logical_not(middle))(lambda: recv(ends.at[0], one_sem.at[cs]))
-
-        def finish(exchange):
-            for_sides(lambda two: sent(exchange[0][0] if two else exchange[0][0].at[0], one_sem.at[exchange[0][2]]))
-            for present, copy in col_copies(*exchange[1]):
-                pl.when(present)(copy.wait_send)
-
-        def relay(what):
-            @pl.when(relays)
-            def _():
-                @pl.loop(0, levels)
-                def _(k):
-                    recv(halo_of[what][1].at[:, k, pl.ds(0, half), :], level_sem.at[halo_of[what][3], k])
-                    relay_copy(what, k).start()
+            pl.when(middle)(lambda: recv(cols_r, col_rs))
+            pl.when(jnp.logical_not(middle))(lambda: recv(cols_r.at[0], col_rs))
+
+        def finish(rows_s, cols_s, row_ss, col_ss):
+            for_sides(lambda two: sent(rows_s if two else rows_s.at[0], one_sem.at[row_ss]))
+            for side, _, present in beside:
+                pl.when(present)(lambda side=side: sent(cols_s, one_sem.at[col_ss + side]))
 
         with scope("t_ready"):
-            start(exchange_a)
+            start(exchange_a())
             pl.semaphore_wait(ready, 1 + lo_n + hi_n)
-        with scope("t_relay"):
-            relay(0)
         with scope("t_xa"):
-            arrive(exchange_a)
+            arrive(row_recv, col_recv, one_sem.at[T_ROW], one_sem.at[T_COL])
 
         def tracer_step(k, cs, u, v, growth, u_lo, u_hi, v_edge, rows_of, packed):
             um, up, vm, vp = 1.0 - u, 1.0 + u, 1.0 - v, 1.0 + v
@@ -431,15 +426,20 @@
                 row_send2[0, k, i] = new[i][0:1]
                 row_send2[1, k, i] = new[i][tile - 1:tile]
             col_send2[k] = pack(new)
-
-        start(exchange_b)
+            start(exchange_b(k))
+
         with scope("t_relay2"):
-            relay(1)
-        with scope('t_xb'):
-            arrive(exchange_b)
+            @pl.when(relays)
+            def _():
+                @pl.loop(0, levels)
+                def _(k):
+                    recv(gmid.at[:, k, pl.ds(0, half), :], level_sem.at[D_MID, k])
+                    relay_copy(k).start()
 
         @pl.loop(0, levels)
         def _(k):
+            with scope("t_xb"):
+                arrive(row_recv2.at[:, k], col_recv2.at[:, k], level_sem.at[T_ROW2, k], level_sem.at[T_COL2, k])
             with scope("t_drive"):
                 for_sides(lambda two: recv(drive.at[k, pl.ds(0, rows_drive + (2 if two else 1))], level_sem.at[T_DRIVE, k]))
             cs = [held[i, k] for i in range(nt)]
@@ -460,13 +460,12 @@
         sent(light_s, one_sem.at[T_LIGHT_S])
         sent(pig_s, one_sem.at[T_PIG_S])
         for_sides(lambda two: sent(pig_s if two else pig_s.at[:, pl.ds(0, half)], one_sem.at[T_SIDE_S]))
-        finish(exchange_a)
-        finish(exchange_b)
+        finish(row_send, col_send, T_ROW_S, T_COL_S)
+        finish(row_send2, col_send2, T_ROW2_S, T_COL2_S)
 
         @pl.when(relays)
         def _():
-            for what in range(2):
-                sent(halo_of[what][1].at[:, :, pl.ds(0, half), :], one_sem.at[(T_HALO_S, T_MID_S)[what]])
+            sent(gmid.at[:, :, pl.ds(0, half), :], one_sem.at[T_MID_S])
 
 
 def write_out(*refs):
@@ -503,7 +502,7 @@
             buf(2, levels, nt, 1, yt), buf(levels, tile, yt), buf(2, levels, nt, 1, yt), buf(2, levels, tile, yt),
             buf(nt, levels, tile, yt), buf(levels, tile, yt),
             buf(levels, 4 * tile, yt), buf(levels, tile, yt),
-            sem(3, levels), sem(N_ONE), pltpu.SemaphoreType.REGULAR,
+            sem(5, levels), sem(N_ONE), pltpu.SemaphoreType.REGULAR,
         ]
         vmem = pl.BlockSpec(memory_space=pltpu.VMEM)
         shapes = [x.shape for x in (flow, chl, tracers, forcing)]

time: 23.7 us -> 22.5 us (0.949)
  Pallas kernels: 22.9 us -> 21.5 us
    pallas_call x1, Pallas kernels: 21.9 us -> 20.6 us  [on_device(): pl.pallas_call(functools.partial(kernel, sizes), out_shape=[pltpu.VMEM(x,...]
where the time goes in v3:
time: 22.5 us; the launch traced here: 22.1 us
  Pallas kernels  21.5 us (96%)
  between operations  0.64 us (3%)
    pallas_call x1, Pallas kernels, on_device(): pl.pallas_call(functools.partial(kernel, sizes), out_shape=[pltpu.VMEM(x,...  20.6 us
    pallas_call x1, Pallas kernels, on_device(): pl.pallas_call(write_out, out_shape=[jax.ShapeDtypeStruct(x, f32) for x i...  0.93 us

profile of v3, /device:TPU:0, one launch (start us, length us, event | category | flops | bytes accessed | tf_op | source)
XLA Modules:
  0.0 22.1 jit_solution(1807143257852312079)
XLA Ops:
  0.6 20.6 %shard_map.102 = (f32[4,6,8,384]{3,2,1,0:T(8,128)S(1)}, f32[6,8,384]{2,1,0:T(8,128)S(1)}, f32[16,6,8,128]{3,2,1,0:T(8,128)S(1)}, f32[4,6,8,128]{3,2,1,0:T(8,128)S(1)}) custom-call(f32[4,6,8,384]{3,2,1,0:T(8,128)} %flow_h.1, f32[6,8,384]{2,1,0:T(8,128)} %chl_h.1, f32[16,6,8,128]{3,2,1,0:T(8,128)} %tracers_h.1, f32[4,6,8,128]{3,2,1,0:T(8,128)} %forcing_h.1, ...), custom_call_target="tpu_custom_call" | custom-call | tf_op jit(solution)/shard_map/pallas_call | solution.py:510
  21.2 0.9 %shard_map.103 = (f32[4,6,8,384]{3,2,1,0:T(8,128)}, f32[6,8,384]{2,1,0:T(8,128)}, f32[16,6,8,128]{3,2,1,0:T(8,128)}, f32[4,6,8,128]{3,2,1,0:T(8,128)}) custom-call(f32[4,6,8,384]{3,2,1,0:T(8,128)S(1)} %get-tuple-element.8.refs_0_, f32[6,8,384]{2,1,0:T(8,128)S(1)} %get-tuple-element.9.refs_1_, f32[16,6,8,128]{3,2,1,0:T(8,128)S(1)} %get-tuple-element.10.refs_2_, ...), custom_call_target="tpu_custom_call" | custom-call | tf_op jit(solution)/shard_map/pallas_call | solution.py:518

commit v4 on v3

--- a/solution.py
+++ b/solution.py
@@ -273,13 +273,20 @@
                 for f in range(4):
                     drive2_send[k, sec, f] = items[f][:, sec * yt:(sec + 1) * yt]
             drive2_copy(k, 0).start()
+
+            @pl.when(strip == 0)
+            def _():
+                for sec in (1, 2):
+                    drive2_copy(k, sec).start()
             for f in range(4):
                 flow_out[f, k] = now[f][0:tile]
 
-        for sec in (1, 2):
-            @pl.loop(0, levels)
-            def _(k):
-                drive2_copy(k, sec).start()
+        @pl.when(has_lo)
+        def _():
+            for sec in (1, 2):
+                @pl.loop(0, levels)
+                def _(k):
+                    drive2_copy(k, sec).start()
 
         with scope("d_light"):
             recv(light_out, one_sem.at[D_LIGHT])
@@ -338,9 +345,7 @@
 
         @pl.loop(0, levels)
         def _(k):
-            items = [tracers[i, k] for i in range(nt)]
-            col_send[k] = pack(items + [forcing[1, k]])
-            for i, x in enumerate(items + [forcing[0, k]]):
+            for i, x in enumerate([tracers[i, k] for i in range(nt)] + [forcing[0, k]]):
                 row_send[0, k, i] = x[0:1]
                 row_send[1, k, i] = x[tile - 1:tile]
 
@@ -349,18 +354,17 @@
         with scope('t_bar'):
             pl.semaphore_wait(barrier, lo_n + hi_n + has_left.astype(jnp.int32) + has_right.astype(jnp.int32))
 
-        def copies(rows_s, rows_r, cols_s, cols_r, row_ss, row_rs, col_ss, col_rs):
+        def row_copies(rows_s, rows_r, row_ss, row_rs):
             for side, offset, present in sides:
                 yield present, remote(rows_s.at[side], rows_r.at[1 - side], one_sem.at[row_ss], row_rs, dev(section, strip + offset))
+
+        def col_copies(cols_s, cols_r, col_ss, col_rs):
             for side, offset, present in beside:
                 yield present, remote(cols_s, cols_r.at[1 - side], one_sem.at[col_ss + side], col_rs, dev(section + offset, strip))
 
-        def exchange_a():
-            return copies(row_send, row_recv, col_send, col_recv, T_ROW_S, one_sem.at[T_ROW], T_COL_S, one_sem.at[T_COL])
-
         def exchange_b(k):
-            return copies(row_send2.at[:, k], row_recv2.at[:, k], col_send2.at[k], col_recv2.at[:, k],
-                          T_ROW2_S, level_sem.at[T_ROW2, k], T_COL2_S, level_sem.at[T_COL2, k])
+            yield from row_copies(row_send2.at[:, k], row_recv2.at[:, k], T_ROW2_S, level_sem.at[T_ROW2, k])
+            yield from col_copies(col_send2.at[k], col_recv2.at[:, k], T_COL2_S, level_sem.at[T_COL2, k])
 
         def start(exchange):
             for present, copy in exchange:
@@ -378,18 +382,24 @@
                 pl.when(present)(lambda side=side: sent(cols_s, one_sem.at[col_ss + side]))
 
         with scope("t_ready"):
-            start(exchange_a())
+            start(row_copies(row_send, row_recv, T_ROW_S, one_sem.at[T_ROW]))
+
+            @pl.loop(0, levels)
+            def _(k):
+                col_send[k] = pack([tracers[i, k] for i in range(nt)] + [forcing[1, k]])
+                start(col_copies(col_send.at[k], col_recv.at[:, k], T_COL_S, one_sem.at[T_COL]))
+
             pl.semaphore_wait(ready, 1 + lo_n + hi_n)
         with scope("t_xa"):
             arrive(row_recv, col_recv, one_sem.at[T_ROW], one_sem.at[T_COL])
 
-        def tracer_step(k, cs, u, v, growth, u_lo, u_hi, v_edge, rows_of, packed):
+        def tracer_step(k, which, cs, u, v, growth, u_lo, u_hi, v_edge, rows_of, packed):
             um, up, vm, vp = 1.0 - u, 1.0 + u, 1.0 - v, 1.0 + v
             hi_m, lo_p = 1.0 - u_hi, 1.0 + u_lo
             edge_m, edge_p = 1.0 - v_edge, 1.0 + v_edge
             wet = k < deep
             out = []
-            for i in range(nt):
+            for i in which:
                 c = cs[i]
                 react = reaction[i, 0] * cs[0]
                 for b in range(1, nt):
@@ -406,21 +416,29 @@
             return ((None, pig_copy(k, section, 0, strip)), (has_lo, pig_copy(k, section, 1, strip - 1)),
                     (has_hi, pig_copy(k, section, 2, strip + 1)))
 
-        @pl.loop(0, levels)
-        def _(k):
+        def step_a(k, which):
             cs = [tracers[i, k] for i in range(nt)]
             packed = jnp.where(odd, col_recv[1, k], col_recv[0, k])
             growth = 0.1 * jnp.exp(0.1 * forcing[2, k] - 0.05 * forcing[3, k])
             v_edge = pltpu.roll(packed, yt - (2 * nt + 1), 1)
-            new = tracer_step(k, cs, forcing[0, k], forcing[1, k], growth, row_recv[0, k, nt], row_recv[1, k, nt], v_edge,
-                              row_recv, packed)
-            pigment = 0.25 * (new[0] * new[0] + new[1] * new[1])
-            pig_s[k] = pigment
+            return tracer_step(k, which, cs, forcing[0, k], forcing[1, k], growth, row_recv[0, k, nt], row_recv[1, k, nt], v_edge,
+                               row_recv, packed)
+
+        @pl.loop(0, levels)
+        def _(k):
+            new = step_a(k, range(2))
+            pig_s[k] = 0.25 * (new[0] * new[0] + new[1] * new[1])
             for present, copy in pig_copies(k):
                 if present is None:
                     copy.start()
                 else:
                     pl.when(present)(copy.start)
+            for i in range(2):
+                held[i, k] = new[i]
+
+        @pl.loop(0, levels)
+        def _(k):
+            new = [held[0, k], held[1, k]] + step_a(k, range(2, nt))
             for i in range(nt):
                 held[i, k] = new[i]
                 row_send2[0, k, i] = new[i][0:1]
@@ -448,7 +466,7 @@
             ends = [jnp.sum(jnp.where(lane == row, drive[k, 3 * tile + at:3 * tile + at + 1], 0.0), axis=1, keepdims=True)
                     for at in range(2)]
             v_edge = jnp.where(lane == 0, ends[1], ends[0])
-            new = tracer_step(k, cs, drive[k, 0:tile], drive[k, tile:2 * tile], growth, drive[k, rows_drive:rows_drive + 1],
+            new = tracer_step(k, range(nt), cs, drive[k, 0:tile], drive[k, tile:2 * tile], growth, drive[k, rows_drive:rows_drive + 1],
                               drive[k, rows_drive + 1:rows_drive + 2], v_edge, row_recv2, packed)
             light_s[k] = 0.25 * (new[0] * new[0] + new[1] * new[1])
             light_copy(k, section, left, strip).start()

time: 22.5 us -> 22.3 us (level); the launches traced: 22.1 us -> 22.2 us
  no operation moved by 1% of the time
where the time goes in v4:
time: 22.3 us; the launch traced here: 22.2 us
  Pallas kernels  21.5 us (96%)
  between operations  0.64 us (3%)
    pallas_call x1, Pallas kernels, on_device(): pl.pallas_call(functools.partial(kernel, sizes), out_shape=[pltpu.VMEM(x,...  20.6 us
    pallas_call x1, Pallas kernels, on_device(): pl.pallas_call(write_out, out_shape=[jax.ShapeDtypeStruct(x, f32) for x i...  0.93 us

profile of v4, /device:TPU:0, one launch (start us, length us, event | category | flops | bytes accessed | tf_op | source)
XLA Modules:
  0.0 22.2 jit_solution(91605048681323477)
XLA Ops:
  0.6 20.6 %shard_map.102 = (f32[4,6,8,384]{3,2,1,0:T(8,128)S(1)}, f32[6,8,384]{2,1,0:T(8,128)S(1)}, f32[16,6,8,128]{3,2,1,0:T(8,128)S(1)}, f32[4,6,8,128]{3,2,1,0:T(8,128)S(1)}) custom-call(f32[4,6,8,384]{3,2,1,0:T(8,128)} %flow_h.1, f32[6,8,384]{2,1,0:T(8,128)} %chl_h.1, f32[16,6,8,128]{3,2,1,0:T(8,128)} %tracers_h.1, f32[4,6,8,128]{3,2,1,0:T(8,128)} %forcing_h.1, ...), custom_call_target="tpu_custom_call" | custom-call | tf_op jit(solution)/shard_map/pallas_call | solution.py:528
  21.2 0.9 %shard_map.103 = (f32[4,6,8,384]{3,2,1,0:T(8,128)}, f32[6,8,384]{2,1,0:T(8,128)}, f32[16,6,8,128]{3,2,1,0:T(8,128)}, f32[4,6,8,128]{3,2,1,0:T(8,128)}) custom-call(f32[4,6,8,384]{3,2,1,0:T(8,128)S(1)} %get-tuple-element.8.refs_0_, f32[6,8,384]{2,1,0:T(8,128)S(1)} %get-tuple-element.9.refs_1_, f32[16,6,8,128]{3,2,1,0:T(8,128)S(1)} %get-tuple-element.10.refs_2_, ...), custom_call_target="tpu_custom_call" | custom-call | tf_op jit(solution)/shard_map/pallas_call | solution.py:536

commit v5 on v4

--- a/solution.py
+++ b/solution.py
@@ -36,19 +36,19 @@
         return col_shift(x, 1, first, -1)
 
     um, up, vm, vp = 1.0 - u, 1.0 + u, 1.0 - v, 1.0 + v
-    new_u = 0.79 * u + 0.1 * v + 0.05 * (row_next(u - p) + row_prev(u + p) + col_next(u) + col_prev(u))
-    new_v = 0.79 * v - 0.1 * u + 0.05 * (row_next(v) + row_prev(v) + col_next(v - p) + col_prev(v + p))
-    new_t = 0.8 * t + 0.05 * (row_next(t * um) + row_prev(t * up) + col_next(t * vm) + col_prev(t * vp)) + heat
-    new_s = 0.8 * s + 0.05 * (row_next(s * um) + row_prev(s * up) + col_next(s * vm) + col_prev(s * vp))
-    return tuple(jnp.where(wet, x, 0.0) for x in (new_u, new_v, new_t, new_s)), p
+    new_u = wet * (15.8 * u + 2.0 * v + (row_next(u - p) + row_prev(u + p) + (col_next(u) + col_prev(u))))
+    new_v = wet * (15.8 * v - 2.0 * u + (row_next(v) + row_prev(v) + (col_next(v - p) + col_prev(v + p))))
+    new_t = wet * (16.0 * t + (row_next(t * um) + row_prev(t * up) + (col_next(t * vm) + col_prev(t * vp)))) + heat
+    new_s = wet * (16.0 * s + (row_next(s * um) + row_prev(s * up) + (col_next(s * vm) + col_prev(s * vp))))
+    return (new_u, new_v, new_t, new_s), p
 
 
 D_HALO, D_MID, D_PIG = 0, 1, 2
 T_DRIVE, T_ROW2, T_COL2 = 2, 3, 4
 D_LIGHT, D_HALO_S, D_MID_S, D_DRIVE_S, D_DRIVE2_S, D_LOAD, D_MASK = range(7)
 (T_ROW, T_COL, T_ROW_S, T_ROW2_S, T_COL_S, T_COL2_S, T_PIG_S, T_SIDE_S, T_LIGHT_S, T_DRIVE2,
- T_LOAD, T_MASK, T_FORCE, T_REACT, T_MID_S) = (0, 1, 2, 3, 4, 6, 8, 9, 10, 11, 12, 13, 14, 15, 16)
-N_ONE = 17
+ T_LOAD, T_MASK, T_FORCE, T_REACT, T_MID_S, T_LEAD, T_LEAD_S, T_EDGE) = (0, 1, 2, 3, 4, 6, 8, 9, 10, 11, 12, 13, 14, 15, 16, 17, 18, 19)
+N_ONE = 21
 
 
 def kernel(sizes, flow_h, chl_h, tracers_h, forcing_h, ocean_h, bottom_h, reaction_h,
@@ -103,7 +103,8 @@
     hi_n = has_hi.astype(jnp.int32)
 
     both = has_lo & has_hi
-    rows_drive = 3 * tile + 2
+    rows_drive = 3 * tile + 1
+    batch = levels // 2 if levels % 2 == 0 else levels
 
     def for_sides(act):
         pl.when(both)(lambda: act(True))
@@ -178,8 +179,10 @@
                           one_sem.at[D_DRIVE_S], level_sem.at[T_DRIVE, k], dev(jnp.int32(sec), strip))
 
         def edge_copy(k, sec, side, offset):
-            return remote(drive_send.at[k, sec, pl.ds(side * (tile - 1), 1)], drive.at[k, pl.ds(rows_drive + 1 - side, 1)],
-                          one_sem.at[D_DRIVE_S], level_sem.at[T_DRIVE, k], dev(jnp.int32(sec), strip + offset))
+            span = pl.ds(k + 1 - batch, batch)
+            return remote(drive_send.at[span, sec, pl.ds(side * (tile - 1), 1)], drive.at[span, pl.ds(rows_drive + 1 - side, 1)],
+                          one_sem.at[D_DRIVE_S], one_sem.at[T_EDGE + lax.div(k, jnp.int32(batch))],
+                          dev(jnp.int32(sec), strip + offset))
 
         def drive2_copy(k, sec):
             return remote(drive2_send.at[k, sec], forcing_out.at[:, k], one_sem.at[D_DRIVE2_S], one_sem.at[T_DRIVE2],
@@ -208,7 +211,8 @@
         tracers_out[...] = jnp.zeros_like(tracers_out)
         forcing_out[...] = jnp.zeros_like(forcing_out)
 
-        on_diagonal = lax.broadcasted_iota(jnp.int32, (tile, yt), 0) == lax.broadcasted_iota(jnp.int32, (tile, yt), 1)
+        lane_row = lax.broadcasted_iota(jnp.int32, (tile, yt), 1) - lax.broadcasted_iota(jnp.int32, (tile, yt), 0)
+        on_diagonal = [lane_row == tile * c for c in range(4)]
         lane_d = lax.broadcasted_iota(jnp.int32, (wide, yt), 1)
 
         def phase(k, now, pigment, sums, opt_s, light_ref):
@@ -218,7 +222,9 @@
             heat = 0.5 * (light_ref[...] - lower)
             opt_s[...] = opt
             light_ref[...] = lower
-            wet = k < depth[...]
+            sea = k < depth[...]
+            wet = jnp.where(sea, 0.05, 0.0)
+            heat = jnp.where(sea, heat, 0.0)
             sum_u = None
             for n in range(SUB):
                 now, p = substep(now, sums[n], heat, wet, first, last, yt)
@@ -240,21 +246,20 @@
                 def _():
                     halo_copy(1, k, side, offset).start()
             mix = 0.1 * now[2][0:tile] - 0.05 * now[3][0:tile]
+            spread = jnp.zeros((tile, yt), jnp.float32)
+            for c, edge in enumerate((yt - 1, yt, 2 * yt - 1, 2 * yt)):
+                spread = jnp.where(on_diagonal[c], mean_v[:, edge:edge + 1], spread)
+            turned = jnp.sum(spread, axis=0, keepdims=True)
             for sec in range(3):
                 here = slice(sec * yt, (sec + 1) * yt)
                 drive_send[k, sec, 0:tile] = mean_u[0:tile, here]
                 drive_send[k, sec, tile:2 * tile] = mean_v[:, here]
                 drive_send[k, sec, 2 * tile:3 * tile] = mix[:, here]
-                for at, edge, inside in ((0, sec * yt - 1, sec > 0), (1, (sec + 1) * yt, sec < 2)):
-                    if inside:
-                        spread = jnp.where(on_diagonal, mean_v[:, edge:edge + 1], 0.0)
-                        drive_send[k, sec, 3 * tile + at:3 * tile + at + 1] = jnp.sum(spread, axis=0, keepdims=True)
-                    else:
-                        drive_send[k, sec, 3 * tile + at:3 * tile + at + 1] = jnp.zeros((1, yt), jnp.float32)
+                drive_send[k, sec, 3 * tile:rows_drive] = turned
             for sec in range(3):
                 drive_copy(k, sec).start()
             for side, offset, present in sides:
-                @pl.when(present)
+                @pl.when(present & (lax.rem(k, jnp.int32(batch)) == batch - 1))
                 def _():
                     for sec in range(3):
                         edge_copy(k, sec, side, offset).start()
@@ -345,7 +350,7 @@
 
         @pl.loop(0, levels)
         def _(k):
-            for i, x in enumerate([tracers[i, k] for i in range(nt)] + [forcing[0, k]]):
+            for i, x in enumerate([forcing[0, k]] + [tracers[i, k] for i in range(nt)]):
                 row_send[0, k, i] = x[0:1]
                 row_send[1, k, i] = x[tile - 1:tile]
 
@@ -370,19 +375,24 @@
             for present, copy in exchange:
                 pl.when(present)(copy.start)
 
-        def arrive(rows_r, cols_r, row_rs, col_rs):
+        def arrive_rows(rows_r, row_rs):
             for_sides(lambda two: recv(rows_r if two else rows_r.at[0], row_rs))
+
+        def arrive_cols(cols_r, col_rs):
             middle = has_left & has_right
             pl.when(middle)(lambda: recv(cols_r, col_rs))
             pl.when(jnp.logical_not(middle))(lambda: recv(cols_r.at[0], col_rs))
 
-        def finish(rows_s, cols_s, row_ss, col_ss):
+        def finish_rows(rows_s, row_ss):
             for_sides(lambda two: sent(rows_s if two else rows_s.at[0], one_sem.at[row_ss]))
+
+        def finish_cols(cols_s, col_ss):
             for side, _, present in beside:
                 pl.when(present)(lambda side=side: sent(cols_s, one_sem.at[col_ss + side]))
 
         with scope("t_ready"):
-            start(row_copies(row_send, row_recv, T_ROW_S, one_sem.at[T_ROW]))
+            for part, send, come in ((pl.ds(0, 3), T_LEAD_S, T_LEAD), (pl.ds(3, nt - 2), T_ROW_S, T_ROW)):
+                start(row_copies(row_send.at[:, :, part], row_recv.at[:, :, part], send, one_sem.at[come]))
 
             @pl.loop(0, levels)
             def _(k):
@@ -391,7 +401,8 @@
 
             pl.semaphore_wait(ready, 1 + lo_n + hi_n)
         with scope("t_xa"):
-            arrive(row_recv, col_recv, one_sem.at[T_ROW], one_sem.at[T_COL])
+            arrive_rows(row_recv.at[:, :, pl.ds(0, 3)], one_sem.at[T_LEAD])
+            arrive_cols(col_recv, one_sem.at[T_COL])
 
         def tracer_step(k, which, cs, u, v, growth, u_lo, u_hi, v_edge, rows_of, packed):
             um, up, vm, vp = 1.0 - u, 1.0 + u, 1.0 - v, 1.0 + v
@@ -421,8 +432,8 @@
             packed = jnp.where(odd, col_recv[1, k], col_recv[0, k])
             growth = 0.1 * jnp.exp(0.1 * forcing[2, k] - 0.05 * forcing[3, k])
             v_edge = pltpu.roll(packed, yt - (2 * nt + 1), 1)
-            return tracer_step(k, which, cs, forcing[0, k], forcing[1, k], growth, row_recv[0, k, nt], row_recv[1, k, nt], v_edge,
-                               row_recv, packed)
+            return tracer_step(k, which, cs, forcing[0, k], forcing[1, k], growth, row_recv[0, k, 0], row_recv[1, k, 0], v_edge,
+                               row_recv.at[:, :, pl.ds(1, nt)], packed)
 
         @pl.loop(0, levels)
         def _(k):
@@ -436,6 +447,9 @@
             for i in range(2):
                 held[i, k] = new[i]
 
+        with scope("t_rest"):
+            arrive_rows(row_recv.at[:, :, pl.ds(3, nt - 2)], one_sem.at[T_ROW])
+
         @pl.loop(0, levels)
         def _(k):
             new = [held[0, k], held[1, k]] + step_a(k, range(2, nt))
@@ -446,7 +460,7 @@
             col_send2[k] = pack(new)
             start(exchange_b(k))
 
-        with scope("t_relay2"):
+        with scope("t_relay"):
             @pl.when(relays)
             def _():
                 @pl.loop(0, levels)
@@ -457,14 +471,21 @@
         @pl.loop(0, levels)
         def _(k):
             with scope("t_xb"):
-                arrive(row_recv2.at[:, k], col_recv2.at[:, k], level_sem.at[T_ROW2, k], level_sem.at[T_COL2, k])
+                arrive_rows(row_recv2.at[:, k], level_sem.at[T_ROW2, k])
+                arrive_cols(col_recv2.at[:, k], level_sem.at[T_COL2, k])
             with scope("t_drive"):
-                for_sides(lambda two: recv(drive.at[k, pl.ds(0, rows_drive + (2 if two else 1))], level_sem.at[T_DRIVE, k]))
+                recv(drive.at[k, pl.ds(0, rows_drive)], level_sem.at[T_DRIVE, k])
+
+                @pl.when(lax.rem(k, jnp.int32(batch)) == 0)
+                def _():
+                    come = one_sem.at[T_EDGE + lax.div(k, jnp.int32(batch))]
+                    for_sides(lambda two: recv(drive.at[pl.ds(k, batch), pl.ds(rows_drive, 2 if two else 1)], come))
             cs = [held[i, k] for i in range(nt)]
             packed = jnp.where(odd, col_recv2[1, k], col_recv2[0, k])
             growth = 0.1 * jnp.exp(drive[k, 2 * tile:3 * tile])
-            ends = [jnp.sum(jnp.where(lane == row, drive[k, 3 * tile + at:3 * tile + at + 1], 0.0), axis=1, keepdims=True)
-                    for at in range(2)]
+            turned = drive[k, 3 * tile:rows_drive]
+            ends = [jnp.sum(jnp.where(lane - row == tile * c, turned, 0.0), axis=1, keepdims=True)
+                    for c in (2 * section - 2, 2 * section + 1)]
             v_edge = jnp.where(lane == 0, ends[1], ends[0])
             new = tracer_step(k, range(nt), cs, drive[k, 0:tile], drive[k, tile:2 * tile], growth, drive[k, rows_drive:rows_drive + 1],
                               drive[k, rows_drive + 1:rows_drive + 2], v_edge, row_recv2, packed)
@@ -478,8 +499,11 @@
         sent(light_s, one_sem.at[T_LIGHT_S])
         sent(pig_s, one_sem.at[T_PIG_S])
         for_sides(lambda two: sent(pig_s if two else pig_s.at[:, pl.ds(0, half)], one_sem.at[T_SIDE_S]))
-        finish(row_send, col_send, T_ROW_S, T_COL_S)
-        finish(row_send2, col_send2, T_ROW2_S, T_COL2_S)
+        finish_rows(row_send.at[:, :, pl.ds(0, 3)], T_LEAD_S)
+        finish_rows(row_send.at[:, :, pl.ds(3, nt - 2)], T_ROW_S)
+        finish_rows(row_send2, T_ROW2_S)
+        finish_cols(col_send, T_COL_S)
+        finish_cols(col_send2, T_COL2_S)
 
         @pl.when(relays)
         def _():

time: 22.3 us -> 22.3 us (level)
  no operation moved by 1% of the time
where the time goes in v5:
time: 22.3 us; the launch traced here: 22 us
  Pallas kernels  21.3 us (96%)
  between operations  0.64 us (3%)
    pallas_call x1, Pallas kernels, on_device(): pl.pallas_call(functools.partial(kernel, sizes), out_shape=[pltpu.VMEM(x,...  20.4 us
    pallas_call x1, Pallas kernels, on_device(): pl.pallas_call(write_out, out_shape=[jax.ShapeDtypeStruct(x, f32) for x i...  0.93 us

profile of v5, /device:TPU:0, one launch (start us, length us, event | category | flops | bytes accessed | tf_op | source)
XLA Modules:
  0.0 22.0 jit_solution(919938229128551995)
XLA Ops:
  0.6 20.4 %shard_map.102 = (f32[4,6,8,384]{3,2,1,0:T(8,128)S(1)}, f32[6,8,384]{2,1,0:T(8,128)S(1)}, f32[16,6,8,128]{3,2,1,0:T(8,128)S(1)}, f32[4,6,8,128]{3,2,1,0:T(8,128)S(1)}) custom-call(f32[4,6,8,384]{3,2,1,0:T(8,128)} %flow_h.1, f32[6,8,384]{2,1,0:T(8,128)} %chl_h.1, f32[16,6,8,128]{3,2,1,0:T(8,128)} %tracers_h.1, f32[4,6,8,128]{3,2,1,0:T(8,128)} %forcing_h.1, ...), custom_call_target="tpu_custom_call" | custom-call | tf_op jit(solution)/shard_map/pallas_call | solution.py:552
  21.1 0.9 %shard_map.103 = (f32[4,6,8,384]{3,2,1,0:T(8,128)}, f32[6,8,384]{2,1,0:T(8,128)}, f32[16,6,8,128]{3,2,1,0:T(8,128)}, f32[4,6,8,128]{3,2,1,0:T(8,128)}) custom-call(f32[4,6,8,384]{3,2,1,0:T(8,128)S(1)} %get-tuple-element.8.refs_0_, f32[6,8,384]{2,1,0:T(8,128)S(1)} %get-tuple-element.9.refs_1_, f32[16,6,8,128]{3,2,1,0:T(8,128)S(1)} %get-tuple-element.10.refs_2_, ...), custom_call_target="tpu_custom_call" | custom-call | tf_op jit(solution)/shard_map/pallas_call | solution.py:560

commit v6 on v5

--- a/solution.py
+++ b/solution.py
@@ -9,6 +9,7 @@
 from jax.sharding import PartitionSpec as P
 
 SUB = 4
+AHEAD = 1
 MESH = pl.DeviceIdType.MESH
 AXES = ("comp", "gy", "gx")
 
@@ -44,11 +45,15 @@
 
 
 D_HALO, D_MID, D_PIG = 0, 1, 2
-T_DRIVE, T_ROW2, T_COL2 = 2, 3, 4
-D_LIGHT, D_HALO_S, D_MID_S, D_DRIVE_S, D_DRIVE2_S, D_LOAD, D_MASK = range(7)
-(T_ROW, T_COL, T_ROW_S, T_ROW2_S, T_COL_S, T_COL2_S, T_PIG_S, T_SIDE_S, T_LIGHT_S, T_DRIVE2,
- T_LOAD, T_MASK, T_FORCE, T_REACT, T_MID_S, T_LEAD, T_LEAD_S, T_EDGE) = (0, 1, 2, 3, 4, 6, 8, 9, 10, 11, 12, 13, 14, 15, 16, 17, 18, 19)
-N_ONE = 21
+T_EDGES2, T_DRIVE = 0, 2
+D_LIGHT, D_LOAD, D_MASK, D_DRIVE_S, D_DRIVE2_S = range(5)
+D_HALO_S, D_MID_S = D_LOAD, D_MASK
+T_ROW, T_COL, T_LEAD, T_DRIVE2, T_EDGE, _, T_LOAD, T_FORCE, T_REACT, T_MASK, T_COL_S, T_COL2_S, T_MID_S, N_ONE = range(14)
+T_ROW_S, T_ROW2_S, T_PIG_S, T_LIGHT_S = T_LOAD, T_FORCE, T_REACT, T_MASK
+
+
+def pair_of(levels):
+    return 2 if levels % 2 == 0 else 1
 
 
 def kernel(sizes, flow_h, chl_h, tracers_h, forcing_h, ocean_h, bottom_h, reaction_h,
@@ -113,7 +118,7 @@
     def pig_copy(k, sec, part, row):
         from_rows = (pl.ds(0, tile), pl.ds(0, half), pl.ds(half, half))[part]
         to_rows = (pl.ds(0, tile), pl.ds(tile, half), pl.ds(tile + half, half))[part]
-        return remote(pig_s.at[k, from_rows], pig.at[sec, k, to_rows], one_sem.at[T_PIG_S if part == 0 else T_SIDE_S],
+        return remote(pig_s.at[k, from_rows], pig.at[sec, k, to_rows], one_sem.at[T_PIG_S],
                       level_sem.at[D_PIG, k], dev(three, row))
 
     def light_copy(k, sec, begin, row):
@@ -279,17 +284,15 @@
                     drive2_send[k, sec, f] = items[f][:, sec * yt:(sec + 1) * yt]
             drive2_copy(k, 0).start()
 
-            @pl.when(strip == 0)
-            def _():
-                for sec in (1, 2):
-                    drive2_copy(k, sec).start()
+            pl.when((k < AHEAD) | (strip == 0))(lambda: drive2_copy(k, 1).start())
+            pl.when(strip == 0)(lambda: drive2_copy(k, 2).start())
             for f in range(4):
                 flow_out[f, k] = now[f][0:tile]
 
         @pl.when(has_lo)
         def _():
-            for sec in (1, 2):
-                @pl.loop(0, levels)
+            for sec, begin in ((1, AHEAD), (2, 0)):
+                @pl.loop(begin, levels)
                 def _(k):
                     drive2_copy(k, sec).start()
 
@@ -365,11 +368,18 @@
 
         def col_copies(cols_s, cols_r, col_ss, col_rs):
             for side, offset, present in beside:
-                yield present, remote(cols_s, cols_r.at[1 - side], one_sem.at[col_ss + side], col_rs, dev(section + offset, strip))
+                yield present, remote(cols_s, cols_r.at[1 - side], one_sem.at[col_ss], col_rs, dev(section + offset, strip))
+
+        joint = pair_of(levels)
+
+        def second_sems(k):
+            at = lax.div(k, jnp.int32(joint))
+            return level_sem.at[T_EDGES2, at], level_sem.at[T_EDGES2, levels // joint + at]
 
         def exchange_b(k):
-            yield from row_copies(row_send2.at[:, k], row_recv2.at[:, k], T_ROW2_S, level_sem.at[T_ROW2, k])
-            yield from col_copies(col_send2.at[k], col_recv2.at[:, k], T_COL2_S, level_sem.at[T_COL2, k])
+            rows_come, cols_come = second_sems(k)
+            yield from row_copies(row_send2.at[:, k], row_recv2.at[:, k], T_ROW2_S, rows_come)
+            yield from col_copies(col_send2.at[k], col_recv2.at[:, k], T_COL2_S, cols_come)
 
         def start(exchange):
             for present, copy in exchange:
@@ -386,12 +396,13 @@
         def finish_rows(rows_s, row_ss):
             for_sides(lambda two: sent(rows_s if two else rows_s.at[0], one_sem.at[row_ss]))
 
-        def finish_cols(cols_s, col_ss):
-            for side, _, present in beside:
-                pl.when(present)(lambda side=side: sent(cols_s, one_sem.at[col_ss + side]))
+        def finish_cols(cols_s, twice, col_ss):
+            middle = has_left & has_right
+            pl.when(middle)(lambda: sent(twice, one_sem.at[col_ss]))
+            pl.when(jnp.logical_not(middle))(lambda: sent(cols_s, one_sem.at[col_ss]))
 
         with scope("t_ready"):
-            for part, send, come in ((pl.ds(0, 3), T_LEAD_S, T_LEAD), (pl.ds(3, nt - 2), T_ROW_S, T_ROW)):
+            for part, send, come in ((pl.ds(0, 3), T_ROW_S, T_LEAD), (pl.ds(3, nt - 2), T_ROW_S, T_ROW)):
                 start(row_copies(row_send.at[:, :, part], row_recv.at[:, :, part], send, one_sem.at[come]))
 
             @pl.loop(0, levels)
@@ -471,8 +482,11 @@
         @pl.loop(0, levels)
         def _(k):
             with scope("t_xb"):
-                arrive_rows(row_recv2.at[:, k], level_sem.at[T_ROW2, k])
-                arrive_cols(col_recv2.at[:, k], level_sem.at[T_COL2, k])
+                @pl.when(lax.rem(k, jnp.int32(joint)) == 0)
+                def _():
+                    rows_come, cols_come = second_sems(k)
+                    arrive_rows(row_recv2.at[:, pl.ds(k, joint)], rows_come)
+                    arrive_cols(col_recv2.at[:, pl.ds(k, joint)], cols_come)
             with scope("t_drive"):
                 recv(drive.at[k, pl.ds(0, rows_drive)], level_sem.at[T_DRIVE, k])
 
@@ -497,13 +511,11 @@
         with scope("t_drive2"):
             recv(forcing_out, one_sem.at[T_DRIVE2])
         sent(light_s, one_sem.at[T_LIGHT_S])
-        sent(pig_s, one_sem.at[T_PIG_S])
-        for_sides(lambda two: sent(pig_s if two else pig_s.at[:, pl.ds(0, half)], one_sem.at[T_SIDE_S]))
-        finish_rows(row_send.at[:, :, pl.ds(0, 3)], T_LEAD_S)
-        finish_rows(row_send.at[:, :, pl.ds(3, nt - 2)], T_ROW_S)
+        for_sides(lambda two: sent(col_recv.at[:, :, pl.ds(0, tile if two else 3 * tile // 4)], one_sem.at[T_PIG_S]))
+        finish_rows(row_send, T_ROW_S)
         finish_rows(row_send2, T_ROW2_S)
-        finish_cols(col_send, T_COL_S)
-        finish_cols(col_send2, T_COL2_S)
+        finish_cols(col_send, col_recv, T_COL_S)
+        finish_cols(col_send2, col_recv2, T_COL2_S)
 
         @pl.when(relays)
         def _():
@@ -544,7 +556,7 @@
             buf(2, levels, nt, 1, yt), buf(levels, tile, yt), buf(2, levels, nt, 1, yt), buf(2, levels, tile, yt),
             buf(nt, levels, tile, yt), buf(levels, tile, yt),
             buf(levels, 4 * tile, yt), buf(levels, tile, yt),
-            sem(5, levels), sem(N_ONE), pltpu.SemaphoreType.REGULAR,
+            sem(3, max(levels, 2 * levels // pair_of(levels))), sem(N_ONE), pltpu.SemaphoreType.REGULAR,
         ]
         vmem = pl.BlockSpec(memory_space=pltpu.VMEM)
         shapes = [x.shape for x in (flow, chl, tracers, forcing)]

time: 22.3 us -> 22 us (0.987)
  no operation moved by 1% of the time
where the time goes in v6:
time: 22 us; the launch traced here: 21.8 us
  Pallas kernels  21.2 us (96%)
  between operations  0.64 us (3%)
    pallas_call x1, Pallas kernels, on_device(): pl.pallas_call(functools.partial(kernel, sizes), out_shape=[pltpu.VMEM(x,...  20.2 us
    pallas_call x1, Pallas kernels, on_device(): pl.pallas_call(write_out, out_shape=[jax.ShapeDtypeStruct(x, f32) for x i...  0.93 us

profile of v6, /device:TPU:0, one launch (start us, length us, event | category | flops | bytes accessed | tf_op | source)
XLA Modules:
  0.0 21.8 jit_solution(15075381274192442259)
XLA Ops:
  0.6 20.2 %shard_map.102 = (f32[4,6,8,384]{3,2,1,0:T(8,128)S(1)}, f32[6,8,384]{2,1,0:T(8,128)S(1)}, f32[16,6,8,128]{3,2,1,0:T(8,128)S(1)}, f32[4,6,8,128]{3,2,1,0:T(8,128)S(1)}) custom-call(f32[4,6,8,384]{3,2,1,0:T(8,128)} %flow_h.1, f32[6,8,384]{2,1,0:T(8,128)} %chl_h.1, f32[16,6,8,128]{3,2,1,0:T(8,128)} %tracers_h.1, f32[4,6,8,128]{3,2,1,0:T(8,128)} %forcing_h.1, ...), custom_call_target="tpu_custom_call" | custom-call | tf_op jit(solution)/shard_map/pallas_call | solution.py:564
  20.9 0.9 %shard_map.103 = (f32[4,6,8,384]{3,2,1,0:T(8,128)}, f32[6,8,384]{2,1,0:T(8,128)}, f32[16,6,8,128]{3,2,1,0:T(8,128)}, f32[4,6,8,128]{3,2,1,0:T(8,128)}) custom-call(f32[4,6,8,384]{3,2,1,0:T(8,128)S(1)} %get-tuple-element.8.refs_0_, f32[6,8,384]{2,1,0:T(8,128)S(1)} %get-tuple-element.9.refs_1_, f32[16,6,8,128]{3,2,1,0:T(8,128)S(1)} %get-tuple-element.10.refs_2_, ...), custom_call_target="tpu_custom_call" | custom-call | tf_op jit(solution)/shard_map/pallas_call | solution.py:572
